TPU v7x, 256 devices: a 4x2x16 block of a 4x16x16 slice. The times are simulated.
256 devices in a mesh: groups: 2 (over y), gx: 128 (over z, x, core).
Axes of the slice: x: 4, y: 2, z: 16, core: 2. Of those that a mesh axis runs over, the one named last changes fastest.
The devices are a block of a 4x16x16 slice.
Arguments:
- pressure: float32 [7, 2048, 128, 128], P(None, ('groups', 'gx')), parts along dimension 1, may hold values from -6 to 6
- adjoint: float32 [7, 2048, 128, 128], P(None, ('groups', 'gx')), parts along dimension 1, may hold values from -6 to 6
- permeability: float32 [3, 2048, 128, 128], P(None, ('groups', 'gx')), parts along dimension 1, may hold values from 0.02 to 40, as said below
- active: int32 [2048, 128, 128], P(('groups', 'gx')), parts along dimension 0, may hold values 0 or 1
- fault_codes: int32 [3, 2048, 128, 128], P(None, ('groups', 'gx')), parts along dimension 1, may hold values from 0 to 3
Outputs:
- gradient: float32 [3, 2048, 128, 128], P(None, ('groups', 'gx')), parts along dimension 1
There are 2 independent parts, one for each index of `groups`. A program takes and returns all parts, laid end to end along the dimension named above; each array names one. Nothing has to cross between parts.
Inputs may be any that keep to these rules, and one draw needn't show every extreme that they name: `permeability`: Positive.
All inputs are finite; a program needn't handle non-finite values. No bound on the sum of `active` on one device may be relied on, other than what follows from the above.
Results may differ from a plain program's by a relative error of at most 0.0003.
Values sent between devices are 32-bit elements; how exact they have to be, the bound alone decides.
A program may use at most 64 MiB of HBM per device.

v0:
```python
import jax
import jax.numpy as jnp
from jax import lax
from jax.sharding import Mesh
from jax.sharding import PartitionSpec as P

GX = ("gx_0", "gx_1", "gx_2")
GROUPS_GX = ("groups", "gx_0", "gx_1", "gx_2")


epsilon = 1e-06


def shifted(value, axis, by):
    count = lax.axis_size(axis)
    pairs = [(i, i + by) for i in range(count) if 0 <= i + by < count]
    return lax.ppermute(value, axis, pairs)


def one_axis_at_a_time(value, axes):
    for axis in axes:
        value = lax.psum(value, axis)
    return value


def multiplier(codes):
    return jnp.where(
        codes == 0, 1.0, jnp.where(codes == 1, 0.6, jnp.where(codes == 2, 0.25, 0.05))
    ).astype(jnp.float32)


def pair_terms(lower_pres, upper_pres, lower_adj, upper_adj, lower_perm, upper_perm, factor):
    products = jnp.sum((lower_adj - upper_adj) * (lower_pres - upper_pres), axis=0)
    summed = lower_perm + upper_perm
    scaled = 2.0 * factor * products / (summed * summed)
    return (scaled * upper_perm * upper_perm, scaled * lower_perm * lower_perm)


def cut(values, start, stop, along):
    return lax.slice_in_dim(values, start, stop, axis=along)


def direction_grad(pressure, adjoint, perm_dir, opened, codes, along):
    count = opened.shape[along]
    factor = (
        multiplier(cut(codes, 0, count - 1, along))
        * cut(opened, 0, count - 1, along)
        * cut(opened, 1, count, along)
    )
    to_lower, to_upper = pair_terms(
        cut(pressure, 0, count - 1, along + 1),
        cut(pressure, 1, count, along + 1),
        cut(adjoint, 0, count - 1, along + 1),
        cut(adjoint, 1, count, along + 1),
        cut(perm_dir, 0, count - 1, along),
        cut(perm_dir, 1, count, along),
        factor,
    )
    widths_lower = [(0, 0), (0, 0), (0, 0)]
    widths_upper = [(0, 0), (0, 0), (0, 0)]
    widths_lower[along] = (0, 1)
    widths_upper[along] = (1, 0)
    return jnp.pad(to_lower, widths_lower) + jnp.pad(to_upper, widths_upper)


def local(pressure, adjoint, permeability, active, fault_codes):
    opened = active.astype(jnp.float32)
    layers = opened.shape[0]
    steps = pressure.shape[0]
    perm_first = permeability[0]
    grad_first = direction_grad(pressure, adjoint, perm_first, opened, fault_codes[0], 0)
    grad_second = direction_grad(pressure, adjoint, permeability[1], opened, fault_codes[1], 1)
    grad_third = direction_grad(pressure, adjoint, permeability[2], opened, fault_codes[2], 2)
    last = layers - 1
    mult_last = multiplier(fault_codes[0, last])
    lowest = jnp.concatenate([pressure[:, 0], adjoint[:, 0], perm_first[0:1], opened[0:1]], axis=0)
    above = shifted(lowest, GX, -1)
    to_lower, outgoing = pair_terms(
        pressure[:, last],
        above[:steps],
        adjoint[:, last],
        above[steps : 2 * steps],
        perm_first[last],
        above[2 * steps],
        mult_last * opened[last] * above[2 * steps + 1],
    )
    to_upper = shifted(outgoing, GX, 1)
    grad_first = grad_first.at[last].add(to_lower)
    grad_first = grad_first.at[0].add(to_upper)
    stacked = jnp.stack(
        [perm_first * grad_first, permeability[1] * grad_second, permeability[2] * grad_third]
    )
    local_sum = jnp.sum(stacked * stacked)
    total = one_axis_at_a_time(local_sum, GX)
    entries = 3 * layers * lax.axis_size(GX) * opened.shape[1] * opened.shape[2]
    root_mean = jnp.sqrt(total / entries + epsilon)
    return stacked / root_mean


def solution(mesh):
    torus = Mesh(
        mesh.devices.reshape(mesh.shape["groups"], 16, 4, 2), ("groups", "gx_0", "gx_1", "gx_2")
    )
    in_specs = (
        P(None, GROUPS_GX, None, None),
        P(None, GROUPS_GX, None, None),
        P(None, GROUPS_GX, None, None),
        P(GROUPS_GX, None, None),
        P(None, GROUPS_GX, None, None),
    )
    out_specs = P(None, GROUPS_GX, None, None)
    return jax.shard_map(local, mesh=torus, in_specs=in_specs, out_specs=out_specs, check_vma=False)
```

profile of v0, /device:TPU:33, one launch (start us, length us, event | category | flops | bytes accessed | tf_op | source)
XLA Modules:
  0.0 94.2 jit_solution(5618692090147059487)
XLA Ops:
  0.0 1.2 %convert_element_type.15 = f32[8,128,128]{2,1,0:T(8,128)S(1)} convert(s32[8,128,128]{2,1,0:T(8,128)} %param.12) | non-fusion elementwise | flops 131072 | bytes 1048576 | tf_op jit(solution)/shard_map/convert_element_type | solution.py:67
  1.3 0.9 slice_bitcast_fusion.6
  2.1 1.2 %slice_bitcast_fusion.4 = (f32[7,128,128]{2,1,0:T(8,128)S(1)}, f32[7,128,128]{2,1,0:T(8,128)S(1)}) fusion(f32[7,8,128,128]{3,2,1,0:T(8,128)} %param.10, f32[7,8,128,128]{3,2,1,0:T(8,128)} %param.9), kind=kLoop, calls=%fused_computation.45 | loop fusion | bytes 1835008 | tf_op jit(solution)/shard_map/squeeze | solution.py:76
  3.3 0.1 pad_maximum_fusion.1
  3.4 22.5 %collective-permute-start = (f32[16,128,128]{2,1,0:T(8,128)S(1)}, f32[16,128,128]{2,1,0:T(8,128)S(1)}, u32[]{:S(2)}, u32[]{:S(2)}) collective-permute-start(f32[16,128,128]{2,1,0:T(8,128)S(1)} %pad_maximum_fusion.1), channel_id=1, source_target_pairs={{1,0},{2,1},{3,2},{4,3},{5,4},{6,5},{7,6},{8,7},{9,8},{10,9},{11,1... | collective-permute-start | bytes 3145736 | tf_op jit(solution)/shard_map/ppermute | solution.py:17
  26.0 4.2 %multiply_reduce_fusion.2 = f32[7,128,128]{2,1,0:T(8,128)S(1)} fusion(f32[7,8,128,128]{3,2,1,0:T(8,128)S(1)} %copy-done, f32[7,8,128,128]{3,2,1,0:T(8,128)} %param.10), kind=kLoop, calls=%fused_computation.2 | loop fusion | flops 3096576 | bytes 13303808 | tf_op jit(solution)/shard_map/reduce_sum | solution.py:33
  30.2 0.1 slice_bitcast_fusion.3
  30.3 2.0 %multiply_reduce_fusion = f32[8,128,127]{2,1,0:T(8,128)S(1)} fusion(f32[7,8,128,128]{3,2,1,0:T(8,128)S(1)} %copy-done, f32[7,8,128,128]{3,2,1,0:T(8,128)S(1)} %copy-done.1), kind=kLoop, calls=%fused_computation | loop fusion | flops 3511296 | bytes 15085568 | tf_op jit(solution)/shard_map/reduce_sum | solution.py:33
  32.3 0.1 slice_bitcast_fusion.2
  32.4 0.2 multiply_multiply_fusion.5
  32.7 0.4 multiply_multiply_fusion.1
  33.1 0.1 multiply_multiply_fusion
  33.2 1.8 %multiply_reduce_fusion.1 = f32[8,127,128]{2,1,0:T(8,128)S(1)} fusion(f32[7,8,128,128]{3,2,1,0:T(8,128)S(1)} %copy-done, f32[7,8,128,128]{3,2,1,0:T(8,128)S(1)} %copy-done.1), kind=kLoop, calls=%fused_computation.1 | loop fusion | flops 3511296 | bytes 15085568 | tf_op jit(solution)/shard_map/reduce_sum | solution.py:33
  35.0 0.3 multiply_multiply_fusion.3
  35.4 0.1 multiply_multiply_fusion.2
  35.5 0.1 fusion.9
  35.6 2.0 %collective-permute-start.1 = (f32[128,128]{1,0:T(8,128)S(1)}, f32[128,128]{1,0:T(8,128)S(1)}, u32[]{:S(2)}, u32[]{:S(2)}) collective-permute-start(f32[128,128]{1,0:T(8,128)S(1)} %multiply_multiply_fusion.6), channel_id=1, source_target_pairs={{0,1},{1,2},{2,3},{3,4},{4,5},{5,6},{6,7},{7,8},{8,9},{9,10},{10,1... | collective-permute-start | bytes 196616 | tf_op jit(solution)/shard_map/ppermute | solution.py:17
  37.6 1.3 %collective-permute-done.1 = f32[128,128]{1,0:T(8,128)S(1)} collective-permute-done((f32[128,128]{1,0:T(8,128)S(1)}, f32[128,128]{1,0:T(8,128)S(1)}, u32[]{:S(2)}, u32[]{:S(2)}) %collective-permute-start.1) | collective-permute-done | bytes 65568 | tf_op jit(solution)/shard_map/ppermute | solution.py:17
  38.9 0.4 fusion.7
  39.3 1.0 %multiply_reduce_fusion.3 = f32[]{:T(128)} fusion(f32[1,8,128,128]{3,2,1,0:T(8,128)S(1)} %get-tuple-element.37, f32[1,8,128,128]{3,2,1,0:T(8,128)S(1)} %get-tuple-element.36, f32[1,8,128,128]{3,2,1,0:T(8,128)S(1)} %get-tuple-element.35), kind=kLoop, calls=%fused_computation.4 | loop fusion | flops 1572863 | bytes 1572868 | tf_op jit(solution)/shard_map/reduce_sum | solution.py:93
  40.3 28.3 %psum.21 = f32[]{:T(128)} all-reduce(f32[]{:T(128)} %multiply_reduce_fusion.3), channel_id=1, replica_groups=mesh['groups'=2,'gx_0'=16,'gx_1'=4,'gx_2'=2] {'gx_0'}, use_global_device_ids=true, to_apply=%region_5.6 | all-reduce | flops 1 | bytes 8 | tf_op jit(solution)/shard_map/psum | solution.py:22
  68.6 8.4 %psum.22 = f32[]{:T(128)} all-reduce(f32[]{:T(128)} %psum.21), channel_id=1, replica_groups=mesh['groups'=2,'gx_0'=16,'gx_1'=4,'gx_2'=2] {'gx_1'}, use_global_device_ids=true, to_apply=%region_6.7 | all-reduce | flops 1 | bytes 8 | tf_op jit(solution)/shard_map/psum | solution.py:22
  77.0 15.2 %psum.23 = f32[]{:T(128)} all-reduce(f32[]{:T(128)} %psum.22), channel_id=1, replica_groups=mesh['groups'=2,'gx_0'=16,'gx_1'=4,'gx_2'=2] {'gx_2'}, use_global_device_ids=true, to_apply=%region_7.8 | all-reduce | flops 1 | bytes 8 | tf_op jit(solution)/shard_map/psum | solution.py:22
  92.8 1.3 %fusion = f32[3,8,128,128]{3,2,1,0:T(8,128)} fusion(f32[1,8,128,128]{3,2,1,0:T(8,128)S(1)} %get-tuple-element.37, f32[1,8,128,128]{3,2,1,0:T(8,128)S(1)} %get-tuple-element.36, f32[1,8,128,128]{3,2,1,0:T(8,128)S(1)} %get-tuple-element.35, f32[]{:T(128)S(6)} %sqrt.3), kind=kLoop, calls=%fused_computation.5 | loop fusion | flops 1179648 | bytes 3145732 | tf_op jit(solution)/shard_map/div | solution.py:97
  (15 shorter events, 0.2 us)
Async XLA Ops:
  0.0 25.9 %copy-start = (f32[7,8,128,128]{3,2,1,0:T(8,128)S(1)}, f32[7,8,128,128]{3,2,1,0:T(8,128)}, u32[]{:S(2)}) copy-start(f32[7,8,128,128]{3,2,1,0:T(8,128)} %param.9) | copy-start | bytes 11010052
  3.4 26.7 %copy-start.2 = (f32[3,8,128,128]{3,2,1,0:T(8,128)S(1)}, f32[3,8,128,128]{3,2,1,0:T(8,128)}, u32[]{:S(2)}) copy-start(f32[3,8,128,128]{3,2,1,0:T(8,128)} %param.11) | copy-start | bytes 4718596
  3.4 32.0 %collective-permute-start = (f32[16,128,128]{2,1,0:T(8,128)S(1)}, f32[16,128,128]{2,1,0:T(8,128)S(1)}, u32[]{:S(2)}, u32[]{:S(2)}) collective-permute-start(f32[16,128,128]{2,1,0:T(8,128)S(1)} %pad_maximum_fusion.1), channel_id=1, source_target_pairs={{1,0},{2,1},{3,2},{4,3},{5,4},{6,5},{7,6},{8,7},{9,8},{10,9},{11,1... | collective-permute-start | bytes 3145736 | tf_op jit(solution)/shard_map/ppermute | solution.py:17
  25.9 4.3 %copy-start.1 = (f32[7,8,128,128]{3,2,1,0:T(8,128)S(1)}, f32[7,8,128,128]{3,2,1,0:T(8,128)}, u32[]{:S(2)}) copy-start(f32[7,8,128,128]{3,2,1,0:T(8,128)} %param.10) | copy-start | bytes 11010052
  30.3 2.0 %copy-start.3 = (s32[3,8,128,128]{3,2,1,0:T(8,128)S(1)}, s32[3,8,128,128]{3,2,1,0:T(8,128)}, u32[]{:S(2)}) copy-start(s32[3,8,128,128]{3,2,1,0:T(8,128)} %param.13) | copy-start | bytes 4718596
  35.6 3.3 %collective-permute-start.1 = (f32[128,128]{1,0:T(8,128)S(1)}, f32[128,128]{1,0:T(8,128)S(1)}, u32[]{:S(2)}, u32[]{:S(2)}) collective-permute-start(f32[128,128]{1,0:T(8,128)S(1)} %multiply_multiply_fusion.6), channel_id=1, source_target_pairs={{0,1},{1,2},{2,3},{3,4},{4,5},{5,6},{6,7},{7,8},{8,9},{9,10},{10,1... | collective-permute-start | bytes 196616 | tf_op jit(solution)/shard_map/ppermute | solution.py:17
where the time goes:
time: 94.4 us; the launch traced here: 94.2 us
  blocking collectives  51.9 us (55%)
  starting transfers between devices  24.4 us (26%)
  other arithmetic  13.4 us (14%)
  local copies, waits for them, and re-layouts  2.28 us (2%)
  waiting for transfers between devices  1.26 us (1%)
    psum x3, blocking collectives, one_axis_at_a_time(): value = lax.psum(value, axis)  51.9 us
    ppermute x2, starting transfers between devices, shifted(): return lax.ppermute(value, axis, pairs)  24.4 us
    reduce_sum x4, other arithmetic, pair_terms(): jnp.sum((lower_adj - upper_adj) * (lower_pres - upper_pres), axis=0)  8.1 us
  transfers between devices with their start and end apart: 2, of which 1 were waited for; matrix products, arithmetic and copies ran while one was open for 10% of the time, Pallas kernels for 0%

commit v1 on v0

v1 whole, which is shorter than its diff:
```python
import functools

import jax
import jax.numpy as jnp
from jax import lax
from jax.experimental import pallas as pl
from jax.experimental.pallas import tpu as pltpu
from jax.sharding import PartitionSpec as P

MESH = pl.DeviceIdType.MESH
F32 = jnp.float32

epsilon = 1e-06

PLANE = 8
BLOCK = 32


def multiplier(codes):
    return jnp.where(codes == 0, 1.0, jnp.where(codes == 1, 0.6, jnp.where(codes == 2, 0.25, 0.05)))


def face(products, factor, lower_perm, upper_perm):
    inverse = 1.0 / (lower_perm + upper_perm)
    weight = (2.0 * factor) * products
    upper = upper_perm * inverse
    lower = lower_perm * inverse
    return weight * upper * upper, weight * lower * lower


def kernel(
    steps, layers, rows, n,
    pres_hbm, adj_hbm, perm_hbm, act_hbm, code_hbm,
    log_ref, inv_ref,
    pres, adj, perm, act, code,
    to_up_x, to_up_y,
    above_pres, above_adj, above_perm, above_act, above_log,
    below_pres, below_adj, below_perm, below_factor, below_log,
    stage_factor, stage_low, stage_high, stage_ra, stage_rb, got_ra, got_rb,
    stage_z, buf_z, stage_p, buf_p,
    load_sem, send_up, recv_up, send_down, recv_down,
    send_z, recv_z, send_p, recv_p, hand,
):
    half = rows // 2
    cells = layers * rows
    top = cells - rows
    planes = n // PLANE
    me = lax.axis_index("gx")
    my_z = me // PLANE
    my_p = lax.rem(me, PLANE)
    up = lax.rem(me + 1, n)
    down = lax.rem(me + n - 1, n)

    def z_peer(by):
        return lax.rem(my_z + planes + by, planes) * PLANE + my_p

    def p_peer(by):
        return my_z * PLANE + lax.rem(my_p + by, PLANE)

    def signal(sem, device):
        pl.semaphore_signal(sem, inc=1, device_id={"gx": device}, device_id_type=MESH)

    barrier = pltpu.get_barrier_semaphore()
    greeted = [up, down, z_peer(1), z_peer(-1)] + [p_peer(by) for by in range(1, PLANE)]
    for device in greeted:
        signal(barrier, device)

    def loads(layer):
        at = pl.ds(layer * rows, rows)
        pairs = [
            (pres_hbm.at[:, at], pres.at[:, at]),
            (adj_hbm.at[:, at], adj.at[:, at]),
            (perm_hbm.at[:, at], perm.at[:, at]),
            (act_hbm.at[at], act.at[at]),
            (code_hbm.at[:, at], code.at[:, at]),
        ]
        return [pltpu.make_async_copy(s, d, load_sem.at[i, layer]) for i, (s, d) in enumerate(pairs)]

    for layer in [0, layers - 1] + list(range(1, layers - 1)):
        for copy in loads(layer):
            copy.start()

    zero8 = jnp.zeros((8, rows), F32)
    for t in range(steps):
        pres[t, pl.ds(cells, 8), :] = zero8
        adj[t, pl.ds(cells, 8), :] = zero8
    for d in range(3):
        perm[d, pl.ds(cells, 8), :] = zero8
    act[pl.ds(cells, 8), :] = jnp.zeros((8, rows), jnp.int32)
    to_up_y[pl.ds(0, 8), :] = zero8

    def arrived(layer):
        for copy in loads(layer):
            copy.wait()

    arrived(0)
    arrived(layers - 1)

    low_a = pl.ds(0, half)
    top_b = pl.ds(top + half, half)

    def remote(src, dst, send, recv, device):
        return pltpu.make_async_remote_copy(
            src_ref=src, dst_ref=dst, send_sem=send, recv_sem=recv,
            device_id={"gx": device}, device_id_type=MESH,
        )

    goes_down = [
        remote(s, d, send_down.at[i], recv_down.at[i], down)
        for i, (s, d) in enumerate([
            (pres.at[:, low_a], above_pres),
            (adj.at[:, low_a], above_adj),
            (perm.at[0, low_a], above_perm),
            (act.at[low_a], above_act),
            (stage_low, above_log),
            (stage_rb, got_rb),
        ])
    ]
    goes_up = [
        remote(s, d, send_up.at[i], recv_up.at[i], up)
        for i, (s, d) in enumerate([
            (pres.at[:, top_b], below_pres),
            (adj.at[:, top_b], below_adj),
            (perm.at[0, top_b], below_perm),
            (stage_factor, below_factor),
            (stage_high, below_log),
            (stage_ra, got_ra),
        ])
    ]
    stage_factor[...] = multiplier(code[0, top_b, :]) * act[top_b, :].astype(F32)

    pl.semaphore_wait(barrier, len(greeted))
    for i in range(2):
        goes_up[i].start()
        goes_down[i].start()
    goes_up[2].start()
    goes_down[2].start()
    goes_down[3].start()

    def shake(round_, by):
        signal(hand.at[round_], z_peer(by))
        signal(hand.at[round_], z_peer(-by))

    shake(0, 1)

    lane = lax.broadcasted_iota(jnp.int32, (BLOCK, rows), 1)
    sub = lax.broadcasted_iota(jnp.int32, (BLOCK, rows), 0)
    z_open = jnp.where(lane == rows - 1, 0.0, 1.0).astype(F32)

    def fold(square):
        return jnp.sum(square.reshape(BLOCK // 8, 8, rows), axis=0)

    def block(start, in_layer, acc, from_below, to_above):
        at = pl.ds(start, BLOCK)
        next_row = pl.ds(start + 1, BLOCK)
        next_layer = pl.ds(start + rows, BLOCK)
        px = py = pz = None
        for t in range(steps):
            p, a = pres[t, at, :], adj[t, at, :]
            y = (a - adj[t, next_row, :]) * (p - pres[t, next_row, :])
            z = (a - pltpu.roll(a, rows - 1, 1)) * (p - pltpu.roll(p, rows - 1, 1))
            py = y if t == 0 else py + y
            pz = z if t == 0 else pz + z
            if to_above:
                x = (a - adj[t, next_layer, :]) * (p - pres[t, next_layer, :])
                px = x if t == 0 else px + x
        opened = act[at, :].astype(F32)

        k = perm[2, at, :]
        factor = multiplier(code[2, at, :]) * opened * pltpu.roll(opened, rows - 1, 1) * z_open
        mine, above = face(pz, factor, k, pltpu.roll(k, rows - 1, 1))
        log = k * (mine + pltpu.roll(above, 1, 1))
        log_ref[2, at, :] = log
        acc = acc + fold(log * log)

        k = perm[1, at, :]
        y_open = jnp.where(in_layer + sub == rows - 1, 0.0, 1.0).astype(F32)
        factor = multiplier(code[1, at, :]) * opened * act[next_row, :].astype(F32) * y_open
        mine, above = face(py, factor, k, perm[1, next_row, :])
        to_up_y[next_row, :] = above
        log = k * (mine + to_up_y[at, :])
        log_ref[1, at, :] = log
        acc = acc + fold(log * log)

        k = perm[0, at, :]
        total = None
        if to_above:
            factor = multiplier(code[0, at, :]) * opened * act[next_layer, :].astype(F32)
            mine, above = face(px, factor, k, perm[0, next_layer, :])
            to_up_x[next_layer, :] = above
            total = mine
        if from_below:
            into = to_up_x[at, :]
            total = into if total is None else total + into
        log = k * total
        log_ref[0, at, :] = log
        if from_below and to_above:
            acc = acc + fold(log * log)
        return acc

    def layer_of(layer, acc, from_below=True, to_above=True):
        def body(i, acc):
            in_layer = pl.multiple_of(i * BLOCK, BLOCK)
            return block(pl.multiple_of(layer * rows + in_layer, BLOCK), in_layer, acc, from_below, to_above)

        return lax.fori_loop(0, rows // BLOCK, body, acc)

    def middle(first, last, acc):
        def body(layer, acc):
            arrived(layer + 1)
            return layer_of(layer, acc)

        return lax.fori_loop(first, last, body, acc)

    arrived(1)
    acc = layer_of(0, jnp.zeros((8, rows), F32), from_below=False)
    stage_low[...] = log_ref[0, low_a, :]
    goes_up[3].start()
    pl.semaphore_wait(hand.at[0], 2)
    shake(1, 2)
    acc = middle(1, 3, acc)
    goes_down[4].start()
    pl.semaphore_wait(hand.at[1], 2)
    shake(2, 4)
    acc = middle(3, layers - 2, acc)
    acc = layer_of(layers - 2, acc)
    stage_high[...] = perm[0, top_b, :] * to_up_x[top_b, :]
    acc = layer_of(layers - 1, acc, to_above=False)
    goes_up[4].start()
    pl.semaphore_wait(hand.at[2], 2)

    not_last = jnp.where(me == n - 1, 0.0, 1.0).astype(F32)
    not_first = jnp.where(me == 0, 0.0, 1.0).astype(F32)

    def products_of(lower_pres, lower_adj, lower_at, upper_pres, upper_adj, upper_at):
        total = None
        for t in range(steps):
            term = (lower_adj[t, lower_at, :] - upper_adj[t, upper_at, :]) * (
                lower_pres[t, lower_at, :] - upper_pres[t, upper_at, :]
            )
            total = term if t == 0 else total + term
        return total

    for i in range(5):
        goes_down[i].wait_recv()
    for i in range(5):
        goes_up[i].wait_recv()

    def shared(i, acc):
        there = pl.ds(pl.multiple_of(i * BLOCK, BLOCK), BLOCK)
        here = pl.ds(pl.multiple_of(top + i * BLOCK, BLOCK), BLOCK)
        products = products_of(pres, adj, here, above_pres, above_adj, there)
        factor = multiplier(code[0, here, :]) * act[here, :].astype(F32) * above_act[there, :].astype(F32) * not_last
        k, k_up = perm[0, here, :], above_perm[there, :]
        mine, other = face(products, factor, k, k_up)
        log = log_ref[0, here, :] + k * mine
        log_ref[0, here, :] = log
        reply = k_up * other
        stage_ra[there, :] = reply
        reply = reply + above_log[there, :]
        acc = acc + fold(log * log) + fold(reply * reply)

        here = pl.ds(pl.multiple_of(half + i * BLOCK, BLOCK), BLOCK)
        products = products_of(below_pres, below_adj, there, pres, adj, here)
        factor = below_factor[there, :] * act[here, :].astype(F32) * not_first
        k, k_low = perm[0, here, :], below_perm[there, :]
        other, mine = face(products, factor, k_low, k)
        log = log_ref[0, here, :] + k * mine
        log_ref[0, here, :] = log
        reply = k_low * other
        stage_rb[there, :] = reply
        reply = reply + below_log[there, :]
        return acc + fold(log * log) + fold(reply * reply)

    acc = lax.fori_loop(0, half // BLOCK, shared, acc)

    def exchange(value, stage, buf, send, recv, mine, count, peer):
        stage[...] = value
        buf[mine] = value
        copies = []
        for by in range(1, count):
            copies.append(
                remote(stage, buf.at[mine], send.at[by], recv.at[by], peer(by))
            )
        order = sorted(range(1, count), key=lambda by: -min(by, count - by))
        for by in order:
            copies[by - 1].start()
        return copies

    copies_z = exchange(
        jnp.sum(acc, axis=0, keepdims=True), stage_z, buf_z, send_z, recv_z, my_z, planes, lambda by: z_peer(by)
    )
    goes_up[5].start()
    goes_down[5].start()
    for copy in copies_z:
        copy.wait_recv()
    copies_p = exchange(
        jnp.sum(buf_z[...], axis=0), stage_p, buf_p, send_p, recv_p, my_p, PLANE, p_peer
    )

    goes_down[5].wait_recv()
    goes_up[5].wait_recv()
    log_ref[0, low_a, :] += got_ra[...]
    log_ref[0, top_b, :] += got_rb[...]

    for copy in copies_p:
        copy.wait_recv()
    total = jnp.sum(jnp.sum(buf_p[...], axis=0), axis=1, keepdims=True)
    entries = 3 * cells * rows * n
    inv_ref[...] = jnp.broadcast_to(1.0 / jnp.sqrt(total / entries + epsilon), inv_ref.shape)

    for copy in copies_z + copies_p + goes_up + goes_down:
        copy.wait_send()


def local(n, pressure, adjoint, permeability, active, fault_codes):
    steps, layers, rows, lanes = pressure.shape
    cells = layers * rows
    half = rows // 2
    planes = n // PLANE
    vmem = pltpu.VMEM
    halo = [
        vmem((steps, half, lanes), F32),
        vmem((steps, half, lanes), F32),
        vmem((half, lanes), F32),
    ]
    tile = vmem((half, lanes), F32)
    scratch = [
        vmem((steps, cells + 8, lanes), F32),
        vmem((steps, cells + 8, lanes), F32),
        vmem((3, cells + 8, lanes), F32),
        vmem((cells + 8, lanes), jnp.int32),
        vmem((3, cells, lanes), jnp.int32),
        vmem((cells, lanes), F32),
        vmem((cells + 8, lanes), F32),
        *halo, vmem((half, lanes), jnp.int32), tile,
        *halo, tile, tile,
        tile, tile, tile, tile, tile, tile, tile,
        vmem((1, lanes), F32), vmem((planes, 1, lanes), F32),
        vmem((1, lanes), F32), vmem((PLANE, 1, lanes), F32),
        pltpu.SemaphoreType.DMA((5, layers)),
        pltpu.SemaphoreType.DMA((6,)), pltpu.SemaphoreType.DMA((6,)),
        pltpu.SemaphoreType.DMA((6,)), pltpu.SemaphoreType.DMA((6,)),
        pltpu.SemaphoreType.DMA((planes,)), pltpu.SemaphoreType.DMA((planes,)),
        pltpu.SemaphoreType.DMA((PLANE,)), pltpu.SemaphoreType.DMA((PLANE,)),
        pltpu.SemaphoreType.REGULAR((3,)),
    ]
    hbm = pl.BlockSpec(memory_space=pltpu.HBM)
    in_hbm = lambda x: pltpu.with_memory_space_constraint(x, pltpu.HBM)
    log, inverse = pl.pallas_call(
        functools.partial(kernel, steps, layers, rows, n),
        out_shape=(
            jax.ShapeDtypeStruct((3, cells, lanes), F32),
            jax.ShapeDtypeStruct((1, lanes), F32),
        ),
        in_specs=[hbm] * 5,
        out_specs=(pl.BlockSpec(memory_space=pltpu.VMEM), pl.BlockSpec(memory_space=pltpu.VMEM)),
        scratch_shapes=scratch,
        compiler_params=pltpu.CompilerParams(
            collective_id=0, has_side_effects=True, vmem_limit_bytes=32 * 1024 * 1024
        ),
        name="gradient",
    )(
        in_hbm(pressure.reshape(steps, cells, lanes)),
        in_hbm(adjoint.reshape(steps, cells, lanes)),
        in_hbm(permeability.reshape(3, cells, lanes)),
        in_hbm(active.reshape(cells, lanes)),
        in_hbm(fault_codes.reshape(3, cells, lanes)),
    )
    out = log * inverse[None]
    return out.reshape(3, layers, rows, lanes)


def solution(mesh):
    n = mesh.shape["gx"]
    whole = ("groups", "gx")
    four = P(None, whole, None, None)
    return jax.shard_map(
        functools.partial(local, n),
        mesh=mesh,
        in_specs=(four, four, four, P(whole, None, None), four),
        out_specs=four,
        check_vma=False,
    )
```

time: 94.4 us -> 45.4 us (0.48)
  blocking collectives: 51.9 us -> 0 us
  Pallas kernels: 0 us -> 44 us
  starting transfers between devices: 24.4 us -> 0 us
  other arithmetic: 13.4 us -> 1.25 us
  local copies, waits for them, and re-layouts: 2.28 us -> 0 us
  waiting for transfers between devices: 1.26 us -> 0 us
    psum x3 -> x0, blocking collectives: 51.9 us -> none  [one_axis_at_a_time(): value = lax.psum(value, axis)]
    pallas_call x0 -> x1, Pallas kernels: none -> 44 us  [local(): pl.pallas_call(functools.partial(kernel, steps, layers, rows, n), out_sha...]
    ppermute x2 -> x0, starting transfers between devices: 24.4 us -> none  [shifted(): return lax.ppermute(value, axis, pairs)]
    reduce_sum x5 -> x0, other arithmetic: 9.1 us -> none  [the longest x4 8.1 us: pair_terms(): jnp.sum((lower_adj - upper_adj) * (lower_pres - upper_pres), axis=0)]
    squeeze x3 -> x0, local copies, waits for them, and re-layouts: 1.4 us -> none  [the longest x1 1.22 us: local(): adjoint[:, 0]]
    div x1 -> x0, other arithmetic: 1.33 us -> none  [local(): return stacked / root_mean]
    ppermute x2 -> x0, waiting for transfers between devices: 1.26 us -> none  [shifted(): return lax.ppermute(value, axis, pairs)]
    convert_element_type x1 -> x0, other arithmetic: 1.23 us -> none  [local(): opened = active.astype(jnp.float32)]
  transfers between devices with their start and end apart: 2 -> 0, of which waited for: 1 -> 0; matrix products, arithmetic and copies ran while one was open for 10% -> 0% of each run, Pallas kernels for 0% -> 0%
where the time goes in v1:
time: 45.4 us; the launch traced here: 45.3 us
  Pallas kernels  44 us (97%)
  other arithmetic  1.25 us (3%)
    pallas_call x1, Pallas kernels, local(): pl.pallas_call(functools.partial(kernel, steps, layers, rows, n), out_sha...  44 us
    mul x1, other arithmetic, local(): out = log * inverse[None]  1.25 us

profile of v1, /device:TPU:33, one launch (start us, length us, event | category | flops | bytes accessed | tf_op | source)
XLA Modules:
  0.0 45.3 jit_solution(7347841134872536351)
XLA Ops:
  0.0 44.0 %gradient.1 = (f32[3,1024,128]{2,1,0:T(8,128)S(1)}, f32[1,128]{1,0:T(1,128)S(1)}) custom-call(f32[7,1024,128]{2,1,0:T(8,128)} %bitcast.8, f32[7,1024,128]{2,1,0:T(8,128)} %bitcast.9, f32[3,1024,128]{2,1,0:T(8,128)} %bitcast.10, s32[1024,128]{1,0:T(8,128)} %bitcast.12, s32[3,1024,128]{2,1,0:T(8,128)} %bitcast.11), custom_call_target="tpu_custom_call" | custom-call | tf_op jit(solution)/shard_map/gradient/pallas_call | solution.py:350
  44.1 1.2 %broadcast_multiply_fusion = f32[3,1024,128]{2,1,0:T(8,128)} fusion(f32[3,1024,128]{2,1,0:T(8,128)S(1)} %get-tuple-element.7, f32[128]{0:T(128)S(1)} %bitcast.7), kind=kLoop, calls=%fused_computation | loop fusion | flops 393216 | bytes 3146240 | tf_op jit(solution)/shard_map/mul | solution.py:370

commit v2 on v1

--- a/solution.py
+++ b/solution.py
@@ -37,36 +37,38 @@
     above_pres, above_adj, above_perm, above_act, above_log,
     below_pres, below_adj, below_perm, below_factor, below_log,
     stage_factor, stage_low, stage_high, stage_ra, stage_rb, got_ra, got_rb,
-    stage_z, buf_z, stage_p, buf_p,
+    stage_sum, sums, stage_inv, got_inv,
     load_sem, send_up, recv_up, send_down, recv_down,
-    send_z, recv_z, send_p, recv_p, hand,
+    send_sum, recv_sum, send_inv, recv_inv,
 ):
     half = rows // 2
     cells = layers * rows
     top = cells - rows
     planes = n // PLANE
     me = lax.axis_index("gx")
-    my_z = me // PLANE
-    my_p = lax.rem(me, PLANE)
+    root = me < PLANE
+    first, last = me == 0, me == n - 1
     up = lax.rem(me + 1, n)
     down = lax.rem(me + n - 1, n)
 
-    def z_peer(by):
-        return lax.rem(my_z + planes + by, planes) * PLANE + my_p
-
-    def p_peer(by):
-        return my_z * PLANE + lax.rem(my_p + by, PLANE)
-
-    def signal(sem, device):
-        pl.semaphore_signal(sem, inc=1, device_id={"gx": device}, device_id_type=MESH)
-
     barrier = pltpu.get_barrier_semaphore()
-    greeted = [up, down, z_peer(1), z_peer(-1)] + [p_peer(by) for by in range(1, PLANE)]
-    for device in greeted:
-        signal(barrier, device)
-
-    def loads(layer):
-        at = pl.ds(layer * rows, rows)
+
+    def greet(device):
+        pl.semaphore_signal(barrier, inc=1, device_id={"gx": device}, device_id_type=MESH)
+
+    @pl.when(jnp.logical_not(last))
+    def _():
+        greet(up)
+
+    @pl.when(jnp.logical_not(first))
+    def _():
+        greet(down)
+
+    groups = [(0, 1), (layers - 1, 1), (1, 1), (2, 2), (4, layers - 5)]
+
+    def loads(group):
+        layer, count = groups[group]
+        at = pl.ds(layer * rows, count * rows)
         pairs = [
             (pres_hbm.at[:, at], pres.at[:, at]),
             (adj_hbm.at[:, at], adj.at[:, at]),
@@ -74,11 +76,24 @@
             (act_hbm.at[at], act.at[at]),
             (code_hbm.at[:, at], code.at[:, at]),
         ]
-        return [pltpu.make_async_copy(s, d, load_sem.at[i, layer]) for i, (s, d) in enumerate(pairs)]
-
-    for layer in [0, layers - 1] + list(range(1, layers - 1)):
-        for copy in loads(layer):
+        return [pltpu.make_async_copy(s, d, load_sem.at[group, i]) for i, (s, d) in enumerate(pairs)]
+
+    loaded = [loads(group) for group in range(len(groups))]
+    for copies in loaded:
+        for copy in copies:
             copy.start()
+
+    def arrived(group):
+        for copy in loaded[group]:
+            copy.wait()
+
+    @pl.when(root)
+    def _():
+        def body(i, carry):
+            greet(lax.rem(me + i, n))
+            return carry
+
+        lax.fori_loop(1, n, body, 0)
 
     zero8 = jnp.zeros((8, rows), F32)
     for t in range(steps):
@@ -89,12 +104,8 @@
     act[pl.ds(cells, 8), :] = jnp.zeros((8, rows), jnp.int32)
     to_up_y[pl.ds(0, 8), :] = zero8
 
-    def arrived(layer):
-        for copy in loads(layer):
-            copy.wait()
-
     arrived(0)
-    arrived(layers - 1)
+    arrived(1)
 
     low_a = pl.ds(0, half)
     top_b = pl.ds(top + half, half)
@@ -129,19 +140,23 @@
     ]
     stage_factor[...] = multiplier(code[0, top_b, :]) * act[top_b, :].astype(F32)
 
-    pl.semaphore_wait(barrier, len(greeted))
-    for i in range(2):
-        goes_up[i].start()
-        goes_down[i].start()
-    goes_up[2].start()
-    goes_down[2].start()
-    goes_down[3].start()
-
-    def shake(round_, by):
-        signal(hand.at[round_], z_peer(by))
-        signal(hand.at[round_], z_peer(-by))
-
-    shake(0, 1)
+    def one_if(condition):
+        return jnp.where(condition, 1, 0)
+
+    pl.semaphore_wait(barrier, 2 + PLANE - one_if(first) - one_if(last) - one_if(root))
+
+    def start(parts):
+        @pl.when(jnp.logical_not(last))
+        def _():
+            for i in parts:
+                goes_up[i].start()
+
+        @pl.when(jnp.logical_not(first))
+        def _():
+            for i in parts:
+                goes_down[i].start()
+
+    start([0, 1, 2, 3])
 
     lane = lax.broadcasted_iota(jnp.int32, (BLOCK, rows), 1)
     sub = lax.broadcasted_iota(jnp.int32, (BLOCK, rows), 0)
@@ -205,32 +220,19 @@
 
         return lax.fori_loop(0, rows // BLOCK, body, acc)
 
-    def middle(first, last, acc):
-        def body(layer, acc):
-            arrived(layer + 1)
-            return layer_of(layer, acc)
-
-        return lax.fori_loop(first, last, body, acc)
-
-    arrived(1)
+    def middle(begin, end, acc):
+        return lax.fori_loop(begin, end, layer_of, acc)
+
+    arrived(2)
     acc = layer_of(0, jnp.zeros((8, rows), F32), from_below=False)
     stage_low[...] = log_ref[0, low_a, :]
-    goes_up[3].start()
-    pl.semaphore_wait(hand.at[0], 2)
-    shake(1, 2)
+    arrived(3)
     acc = middle(1, 3, acc)
-    goes_down[4].start()
-    pl.semaphore_wait(hand.at[1], 2)
-    shake(2, 4)
-    acc = middle(3, layers - 2, acc)
-    acc = layer_of(layers - 2, acc)
+    arrived(4)
+    acc = middle(3, layers - 1, acc)
     stage_high[...] = perm[0, top_b, :] * to_up_x[top_b, :]
     acc = layer_of(layers - 1, acc, to_above=False)
-    goes_up[4].start()
-    pl.semaphore_wait(hand.at[2], 2)
-
-    not_last = jnp.where(me == n - 1, 0.0, 1.0).astype(F32)
-    not_first = jnp.where(me == 0, 0.0, 1.0).astype(F32)
+    start([4])
 
     def products_of(lower_pres, lower_adj, lower_at, upper_pres, upper_adj, upper_at):
         total = None
@@ -241,76 +243,114 @@
             total = term if t == 0 else total + term
         return total
 
-    for i in range(5):
-        goes_down[i].wait_recv()
-    for i in range(5):
-        goes_up[i].wait_recv()
+    def received(parts):
+        @pl.when(jnp.logical_not(last))
+        def _():
+            for i in parts:
+                goes_down[i].wait_recv()
+
+        @pl.when(jnp.logical_not(first))
+        def _():
+            for i in parts:
+                goes_up[i].wait_recv()
+
+    received(range(5))
+
+    def keep(condition, value):
+        return jnp.where(condition, value, 0.0)
 
     def shared(i, acc):
         there = pl.ds(pl.multiple_of(i * BLOCK, BLOCK), BLOCK)
         here = pl.ds(pl.multiple_of(top + i * BLOCK, BLOCK), BLOCK)
+        inside = jnp.logical_not(last)
         products = products_of(pres, adj, here, above_pres, above_adj, there)
-        factor = multiplier(code[0, here, :]) * act[here, :].astype(F32) * above_act[there, :].astype(F32) * not_last
+        factor = multiplier(code[0, here, :]) * act[here, :].astype(F32) * above_act[there, :].astype(F32)
         k, k_up = perm[0, here, :], above_perm[there, :]
         mine, other = face(products, factor, k, k_up)
-        log = log_ref[0, here, :] + k * mine
+        log = log_ref[0, here, :] + keep(inside, k * mine)
         log_ref[0, here, :] = log
         reply = k_up * other
         stage_ra[there, :] = reply
-        reply = reply + above_log[there, :]
-        acc = acc + fold(log * log) + fold(reply * reply)
+        reply = keep(inside, reply + above_log[there, :])
+        end = keep(last, log_ref[0, pl.ds(pl.multiple_of(top + half + i * BLOCK, BLOCK), BLOCK), :])
+        acc = acc + fold(log * log) + fold(reply * reply) + fold(end * end)
 
         here = pl.ds(pl.multiple_of(half + i * BLOCK, BLOCK), BLOCK)
+        inside = jnp.logical_not(first)
         products = products_of(below_pres, below_adj, there, pres, adj, here)
-        factor = below_factor[there, :] * act[here, :].astype(F32) * not_first
+        factor = below_factor[there, :] * act[here, :].astype(F32)
         k, k_low = perm[0, here, :], below_perm[there, :]
         other, mine = face(products, factor, k_low, k)
-        log = log_ref[0, here, :] + k * mine
+        log = log_ref[0, here, :] + keep(inside, k * mine)
         log_ref[0, here, :] = log
         reply = k_low * other
         stage_rb[there, :] = reply
-        reply = reply + below_log[there, :]
-        return acc + fold(log * log) + fold(reply * reply)
+        reply = keep(inside, reply + below_log[there, :])
+        end = keep(first, log_ref[0, there, :])
+        return acc + fold(log * log) + fold(reply * reply) + fold(end * end)
 
     acc = lax.fori_loop(0, half // BLOCK, shared, acc)
 
-    def exchange(value, stage, buf, send, recv, mine, count, peer):
-        stage[...] = value
-        buf[mine] = value
-        copies = []
-        for by in range(1, count):
-            copies.append(
-                remote(stage, buf.at[mine], send.at[by], recv.at[by], peer(by))
-            )
-        order = sorted(range(1, count), key=lambda by: -min(by, count - by))
-        for by in order:
-            copies[by - 1].start()
-        return copies
-
-    copies_z = exchange(
-        jnp.sum(acc, axis=0, keepdims=True), stage_z, buf_z, send_z, recv_z, my_z, planes, lambda by: z_peer(by)
-    )
-    goes_up[5].start()
-    goes_down[5].start()
-    for copy in copies_z:
-        copy.wait_recv()
-    copies_p = exchange(
-        jnp.sum(buf_z[...], axis=0), stage_p, buf_p, send_p, recv_p, my_p, PLANE, p_peer
-    )
-
-    goes_down[5].wait_recv()
-    goes_up[5].wait_recv()
-    log_ref[0, low_a, :] += got_ra[...]
-    log_ref[0, top_b, :] += got_rb[...]
-
-    for copy in copies_p:
-        copy.wait_recv()
-    total = jnp.sum(jnp.sum(buf_p[...], axis=0), axis=1, keepdims=True)
-    entries = 3 * cells * rows * n
-    inv_ref[...] = jnp.broadcast_to(1.0 / jnp.sqrt(total / entries + epsilon), inv_ref.shape)
-
-    for copy in copies_z + copies_p + goes_up + goes_down:
-        copy.wait_send()
+    partial = jnp.sum(acc, axis=0, keepdims=True)
+    stage_sum[...] = partial
+    to_roots = [
+        remote(stage_sum, sums.at[me], send_sum.at[q], recv_sum, q) for q in range(PLANE)
+    ]
+    for q in range(PLANE):
+        @pl.when(me != q)
+        def _():
+            to_roots[q].start()
+
+    start([5])
+    received([5])
+
+    @pl.when(jnp.logical_not(first))
+    def _():
+        log_ref[0, low_a, :] += got_ra[...]
+
+    @pl.when(jnp.logical_not(last))
+    def _():
+        log_ref[0, top_b, :] += got_rb[...]
+
+    @pl.when(root)
+    def _():
+        sums[me] = partial
+        others = sums.at[pl.ds(0, n - 1)]
+        pltpu.make_async_copy(others, others, recv_sum).wait()
+        quarter = n // 4
+        total = sum(jnp.sum(sums[pl.ds(q * quarter, quarter)], axis=0) for q in range(4))
+        total = jnp.sum(total, axis=1, keepdims=True)
+        entries = 3 * cells * rows * n
+        inverse = jnp.broadcast_to(1.0 / jnp.sqrt(total / entries + epsilon), inv_ref.shape)
+        stage_inv[...] = inverse
+        copies = [
+            remote(stage_inv, got_inv, send_inv.at[z], recv_inv, me + z * PLANE) for z in range(1, planes)
+        ]
+        for copy in copies:
+            copy.start()
+        inv_ref[...] = inverse
+        for copy in copies:
+            copy.wait_send()
+
+    @pl.when(jnp.logical_not(root))
+    def _():
+        remote(stage_inv, got_inv, send_inv.at[0], recv_inv, me).wait_recv()
+        inv_ref[...] = got_inv[...]
+
+    for q in range(PLANE):
+        @pl.when(me != q)
+        def _():
+            to_roots[q].wait_send()
+
+    @pl.when(jnp.logical_not(last))
+    def _():
+        for copy in goes_up:
+            copy.wait_send()
+
+    @pl.when(jnp.logical_not(first))
+    def _():
+        for copy in goes_down:
+            copy.wait_send()
 
 
 def local(n, pressure, adjoint, permeability, active, fault_codes):
@@ -336,14 +376,13 @@
         *halo, vmem((half, lanes), jnp.int32), tile,
         *halo, tile, tile,
         tile, tile, tile, tile, tile, tile, tile,
-        vmem((1, lanes), F32), vmem((planes, 1, lanes), F32),
-        vmem((1, lanes), F32), vmem((PLANE, 1, lanes), F32),
-        pltpu.SemaphoreType.DMA((5, layers)),
+        vmem((1, lanes), F32), vmem((n, 1, lanes), F32),
+        vmem((1, lanes), F32), vmem((1, lanes), F32),
+        pltpu.SemaphoreType.DMA((5, 5)),
         pltpu.SemaphoreType.DMA((6,)), pltpu.SemaphoreType.DMA((6,)),
         pltpu.SemaphoreType.DMA((6,)), pltpu.SemaphoreType.DMA((6,)),
-        pltpu.SemaphoreType.DMA((planes,)), pltpu.SemaphoreType.DMA((planes,)),
-        pltpu.SemaphoreType.DMA((PLANE,)), pltpu.SemaphoreType.DMA((PLANE,)),
-        pltpu.SemaphoreType.REGULAR((3,)),
+        pltpu.SemaphoreType.DMA((PLANE,)), pltpu.SemaphoreType.DMA,
+        pltpu.SemaphoreType.DMA((planes,)), pltpu.SemaphoreType.DMA,
     ]
     hbm = pl.BlockSpec(memory_space=pltpu.HBM)
     in_hbm = lambda x: pltpu.with_memory_space_constraint(x, pltpu.HBM)

time: 45.4 us -> 49.8 us (1.097)
  Pallas kernels: 44 us -> 48.5 us
    pallas_call x1, Pallas kernels: 44 us -> 48.5 us  [local(): pl.pallas_call(functools.partial(kernel, steps, layers, rows, n), out_sha...]
where the time goes in v2:
time: 49.8 us; the launch traced here: 49.7 us
  Pallas kernels  48.5 us (97%)
  other arithmetic  1.25 us (3%)
    pallas_call x1, Pallas kernels, local(): pl.pallas_call(functools.partial(kernel, steps, layers, rows, n), out_sha...  48.5 us
    mul x1, other arithmetic, local(): out = log * inverse[None]  1.25 us

profile of v2, /device:TPU:33, one launch (start us, length us, event | category | flops | bytes accessed | tf_op | source)
XLA Modules:
  0.0 49.7 jit_solution(8117750586791069777)
XLA Ops:
  0.0 48.5 %gradient.1 = (f32[3,1024,128]{2,1,0:T(8,128)S(1)}, f32[1,128]{1,0:T(1,128)S(1)}) custom-call(f32[7,1024,128]{2,1,0:T(8,128)} %bitcast.8, f32[7,1024,128]{2,1,0:T(8,128)} %bitcast.9, f32[3,1024,128]{2,1,0:T(8,128)} %bitcast.10, s32[1024,128]{1,0:T(8,128)} %bitcast.12, s32[3,1024,128]{2,1,0:T(8,128)} %bitcast.11), custom_call_target="tpu_custom_call" | custom-call | tf_op jit(solution)/shard_map/gradient/pallas_call | solution.py:389
  48.5 1.2 %broadcast_multiply_fusion = f32[3,1024,128]{2,1,0:T(8,128)} fusion(f32[3,1024,128]{2,1,0:T(8,128)S(1)} %get-tuple-element.7, f32[128]{0:T(128)S(1)} %bitcast.7), kind=kLoop, calls=%fused_computation | loop fusion | flops 393216 | bytes 3146240 | tf_op jit(solution)/shard_map/mul | solution.py:409

commit v3 on v2

--- a/solution.py
+++ b/solution.py
@@ -34,22 +34,40 @@
     log_ref, inv_ref,
     pres, adj, perm, act, code,
     to_up_x, to_up_y,
-    above_pres, above_adj, above_perm, above_act, above_log,
+    above_pres, above_adj, above_perm, above_log,
     below_pres, below_adj, below_perm, below_factor, below_log,
-    stage_factor, stage_low, stage_high, stage_ra, stage_rb, got_ra, got_rb,
+    stage_factor, stage_perm, stage_low, stage_high, stage_ra, stage_rb, got_ra, got_rb,
     stage_sum, sums, stage_inv, got_inv,
     load_sem, send_up, recv_up, send_down, recv_down,
-    send_sum, recv_sum, send_inv, recv_inv,
+    send_sum, recv_sum, send_inv, send_extra, recv_inv,
 ):
     half = rows // 2
     cells = layers * rows
     top = cells - rows
     planes = n // PLANE
+    takers = 2 * PLANE - 1
     me = lax.axis_index("gx")
-    root = me < PLANE
     first, last = me == 0, me == n - 1
-    up = lax.rem(me + 1, n)
-    down = lax.rem(me + n - 1, n)
+    taker = jnp.logical_and(me >= 1, me <= takers)
+    up, down = me + 1, me - 1
+
+    def wait_rows(sem, row_count, wide=1):
+        ref = pres.at[pl.ds(0, wide), pl.ds(0, row_count // wide)]
+        pltpu.make_async_copy(ref, ref, sem).wait()
+
+    def load(group, parts):
+        for src, dst, begin, count in parts:
+            at = pl.ds(begin, count)
+            where = (at,) if len(src.shape) == 2 else (slice(None), at)
+            pltpu.make_async_copy(src.at[where], dst.at[where], load_sem.at[group]).start()
+
+    fields = [(pres_hbm, pres), (adj_hbm, adj)]
+    others = [(perm_hbm, perm), (act_hbm, act), (code_hbm, code)]
+
+    def span(refs, begin, end):
+        return [(src, dst, begin, end - begin) for src, dst in refs]
+
+    load(0, span(fields, 0, half) + span(fields, top + half, cells))
 
     barrier = pltpu.get_barrier_semaphore()
 
@@ -64,36 +82,16 @@
     def _():
         greet(down)
 
-    groups = [(0, 1), (layers - 1, 1), (1, 1), (2, 2), (4, layers - 5)]
-
-    def loads(group):
-        layer, count = groups[group]
-        at = pl.ds(layer * rows, count * rows)
-        pairs = [
-            (pres_hbm.at[:, at], pres.at[:, at]),
-            (adj_hbm.at[:, at], adj.at[:, at]),
-            (perm_hbm.at[:, at], perm.at[:, at]),
-            (act_hbm.at[at], act.at[at]),
-            (code_hbm.at[:, at], code.at[:, at]),
-        ]
-        return [pltpu.make_async_copy(s, d, load_sem.at[group, i]) for i, (s, d) in enumerate(pairs)]
-
-    loaded = [loads(group) for group in range(len(groups))]
-    for copies in loaded:
-        for copy in copies:
-            copy.start()
-
-    def arrived(group):
-        for copy in loaded[group]:
-            copy.wait()
-
-    @pl.when(root)
-    def _():
-        def body(i, carry):
-            greet(lax.rem(me + i, n))
+    @pl.when(taker)
+    def _():
+        def body(device, carry):
+            @pl.when(device != me)
+            def _():
+                greet(device)
+
             return carry
 
-        lax.fori_loop(1, n, body, 0)
+        lax.fori_loop(0, n, body, 0)
 
     zero8 = jnp.zeros((8, rows), F32)
     for t in range(steps):
@@ -104,9 +102,6 @@
     act[pl.ds(cells, 8), :] = jnp.zeros((8, rows), jnp.int32)
     to_up_y[pl.ds(0, 8), :] = zero8
 
-    arrived(0)
-    arrived(1)
-
     low_a = pl.ds(0, half)
     top_b = pl.ds(top + half, half)
 
@@ -117,18 +112,17 @@
         )
 
     goes_down = [
-        remote(s, d, send_down.at[i], recv_down.at[i], down)
+        remote(s, d, send_down, recv_down.at[int(i == 4)], down)
         for i, (s, d) in enumerate([
             (pres.at[:, low_a], above_pres),
             (adj.at[:, low_a], above_adj),
-            (perm.at[0, low_a], above_perm),
-            (act.at[low_a], above_act),
+            (stage_perm, above_perm),
             (stage_low, above_log),
             (stage_rb, got_rb),
         ])
     ]
     goes_up = [
-        remote(s, d, send_up.at[i], recv_up.at[i], up)
+        remote(s, d, send_up, recv_up.at[int(i == 5)], up)
         for i, (s, d) in enumerate([
             (pres.at[:, top_b], below_pres),
             (adj.at[:, top_b], below_adj),
@@ -138,25 +132,33 @@
             (stage_ra, got_ra),
         ])
     ]
-    stage_factor[...] = multiplier(code[0, top_b, :]) * act[top_b, :].astype(F32)
-
-    def one_if(condition):
-        return jnp.where(condition, 1, 0)
-
-    pl.semaphore_wait(barrier, 2 + PLANE - one_if(first) - one_if(last) - one_if(root))
-
-    def start(parts):
+
+    def start_up(*parts):
         @pl.when(jnp.logical_not(last))
         def _():
             for i in parts:
                 goes_up[i].start()
 
+    def start_down(*parts):
         @pl.when(jnp.logical_not(first))
         def _():
             for i in parts:
                 goes_down[i].start()
 
-    start([0, 1, 2, 3])
+    def one_if(condition):
+        return jnp.where(condition, 1, 0)
+
+    wait_rows(load_sem.at[0], 4 * steps * half, steps)
+    pl.semaphore_wait(barrier, 2 + takers - one_if(first) - one_if(last) - one_if(taker))
+    start_up(0, 1)
+    start_down(0, 1)
+
+    load(1, span(fields, half, 2 * rows) + span(others, 0, 2 * rows))
+    load(2, span(fields + others, 2 * rows, 4 * rows))
+    load(3, span(fields + others, 4 * rows, 6 * rows))
+    load(4, span(fields, 6 * rows, top + half) + span(others, 6 * rows, cells))
+    edge = 2 * steps * (2 * rows - half) + 7 * 2 * rows
+    whole = (2 * steps + 7) * 2 * rows
 
     lane = lax.broadcasted_iota(jnp.int32, (BLOCK, rows), 1)
     sub = lax.broadcasted_iota(jnp.int32, (BLOCK, rows), 0)
@@ -223,16 +225,24 @@
     def middle(begin, end, acc):
         return lax.fori_loop(begin, end, layer_of, acc)
 
-    arrived(2)
+    wait_rows(load_sem.at[1], edge, steps)
+    stage_perm[...] = perm[0, low_a, :] * act[low_a, :].astype(F32)
     acc = layer_of(0, jnp.zeros((8, rows), F32), from_below=False)
+    start_down(2)
     stage_low[...] = log_ref[0, low_a, :]
-    arrived(3)
+    wait_rows(load_sem.at[2], whole, steps)
     acc = middle(1, 3, acc)
-    arrived(4)
-    acc = middle(3, layers - 1, acc)
+    start_down(3)
+    wait_rows(load_sem.at[3], whole, steps)
+    acc = middle(3, 5, acc)
+    wait_rows(load_sem.at[4], edge, steps)
+    start_up(2)
+    stage_factor[...] = multiplier(code[0, top_b, :]) * act[top_b, :].astype(F32)
+    acc = middle(5, layers - 1, acc)
+    start_up(3)
     stage_high[...] = perm[0, top_b, :] * to_up_x[top_b, :]
     acc = layer_of(layers - 1, acc, to_above=False)
-    start([4])
+    start_up(4)
 
     def products_of(lower_pres, lower_adj, lower_at, upper_pres, upper_adj, upper_at):
         total = None
@@ -243,18 +253,13 @@
             total = term if t == 0 else total + term
         return total
 
-    def received(parts):
-        @pl.when(jnp.logical_not(last))
-        def _():
-            for i in parts:
-                goes_down[i].wait_recv()
-
-        @pl.when(jnp.logical_not(first))
-        def _():
-            for i in parts:
-                goes_up[i].wait_recv()
-
-    received(range(5))
+    @pl.when(jnp.logical_not(last))
+    def _():
+        wait_rows(recv_down.at[0], (2 * steps + 2) * half, 2)
+
+    @pl.when(jnp.logical_not(first))
+    def _():
+        wait_rows(recv_up.at[0], (2 * steps + 3) * half, 2)
 
     def keep(condition, value):
         return jnp.where(condition, value, 0.0)
@@ -264,7 +269,7 @@
         here = pl.ds(pl.multiple_of(top + i * BLOCK, BLOCK), BLOCK)
         inside = jnp.logical_not(last)
         products = products_of(pres, adj, here, above_pres, above_adj, there)
-        factor = multiplier(code[0, here, :]) * act[here, :].astype(F32) * above_act[there, :].astype(F32)
+        factor = multiplier(code[0, here, :]) * act[here, :].astype(F32)
         k, k_up = perm[0, here, :], above_perm[there, :]
         mine, other = face(products, factor, k, k_up)
         log = log_ref[0, here, :] + keep(inside, k * mine)
@@ -293,64 +298,66 @@
 
     partial = jnp.sum(acc, axis=0, keepdims=True)
     stage_sum[...] = partial
-    to_roots = [
-        remote(stage_sum, sums.at[me], send_sum.at[q], recv_sum, q) for q in range(PLANE)
-    ]
-    for q in range(PLANE):
-        @pl.when(me != q)
-        def _():
-            to_roots[q].start()
-
-    start([5])
-    received([5])
+    to_takers = [remote(stage_sum, sums.at[me], send_sum, recv_sum, q) for q in range(1, takers + 1)]
+
+    @pl.when(jnp.logical_not(taker))
+    def _():
+        for copy in to_takers:
+            copy.start()
+
+    @pl.when(taker)
+    def _():
+        for q in range(1, takers + 1):
+            @pl.when(me != q)
+            def _():
+                to_takers[q - 1].start()
+
+    start_up(5)
+    start_down(4)
 
     @pl.when(jnp.logical_not(first))
     def _():
+        wait_rows(recv_up.at[1], half)
         log_ref[0, low_a, :] += got_ra[...]
+        wait_rows(send_down, (2 * steps + 3) * half, 2)
 
     @pl.when(jnp.logical_not(last))
     def _():
+        wait_rows(recv_down.at[1], half)
         log_ref[0, top_b, :] += got_rb[...]
-
-    @pl.when(root)
-    def _():
+        wait_rows(send_up, (2 * steps + 4) * half, 2)
+
+    @pl.when(taker)
+    def _():
+        wait_rows(send_sum, takers - 1)
         sums[me] = partial
-        others = sums.at[pl.ds(0, n - 1)]
-        pltpu.make_async_copy(others, others, recv_sum).wait()
+        wait_rows(recv_sum, n - 1)
         quarter = n // 4
         total = sum(jnp.sum(sums[pl.ds(q * quarter, quarter)], axis=0) for q in range(4))
         total = jnp.sum(total, axis=1, keepdims=True)
         entries = 3 * cells * rows * n
         inverse = jnp.broadcast_to(1.0 / jnp.sqrt(total / entries + epsilon), inv_ref.shape)
-        stage_inv[...] = inverse
-        copies = [
-            remote(stage_inv, got_inv, send_inv.at[z], recv_inv, me + z * PLANE) for z in range(1, planes)
-        ]
-        for copy in copies:
-            copy.start()
         inv_ref[...] = inverse
-        for copy in copies:
-            copy.wait_send()
-
-    @pl.when(jnp.logical_not(root))
-    def _():
-        remote(stage_inv, got_inv, send_inv.at[0], recv_inv, me).wait_recv()
+
+        @pl.when(me >= PLANE)
+        def _():
+            stage_inv[...] = inverse
+            for z in range(1, planes - 1):
+                remote(stage_inv, got_inv, send_inv, recv_inv, me + z * PLANE).start()
+            to_first = remote(stage_inv, got_inv, send_extra, recv_inv, 0)
+
+            @pl.when(me == PLANE)
+            def _():
+                to_first.start()
+                to_first.wait_send()
+
+            wait_rows(send_inv, planes - 2)
+
+    @pl.when(jnp.logical_not(taker))
+    def _():
+        wait_rows(send_sum, takers)
+        wait_rows(recv_inv, 1)
         inv_ref[...] = got_inv[...]
-
-    for q in range(PLANE):
-        @pl.when(me != q)
-        def _():
-            to_roots[q].wait_send()
-
-    @pl.when(jnp.logical_not(last))
-    def _():
-        for copy in goes_up:
-            copy.wait_send()
-
-    @pl.when(jnp.logical_not(first))
-    def _():
-        for copy in goes_down:
-            copy.wait_send()
 
 
 def local(n, pressure, adjoint, permeability, active, fault_codes):
@@ -358,7 +365,7 @@
     cells = layers * rows
     half = rows // 2
     planes = n // PLANE
-    vmem = pltpu.VMEM
+    vmem, dma = pltpu.VMEM, pltpu.SemaphoreType.DMA
     halo = [
         vmem((steps, half, lanes), F32),
         vmem((steps, half, lanes), F32),
@@ -373,16 +380,13 @@
         vmem((3, cells, lanes), jnp.int32),
         vmem((cells, lanes), F32),
         vmem((cells + 8, lanes), F32),
-        *halo, vmem((half, lanes), jnp.int32), tile,
+        *halo, tile,
         *halo, tile, tile,
-        tile, tile, tile, tile, tile, tile, tile,
+        tile, tile, tile, tile, tile, tile, tile, tile,
         vmem((1, lanes), F32), vmem((n, 1, lanes), F32),
         vmem((1, lanes), F32), vmem((1, lanes), F32),
-        pltpu.SemaphoreType.DMA((5, 5)),
-        pltpu.SemaphoreType.DMA((6,)), pltpu.SemaphoreType.DMA((6,)),
-        pltpu.SemaphoreType.DMA((6,)), pltpu.SemaphoreType.DMA((6,)),
-        pltpu.SemaphoreType.DMA((PLANE,)), pltpu.SemaphoreType.DMA,
-        pltpu.SemaphoreType.DMA((planes,)), pltpu.SemaphoreType.DMA,
+        dma((5,)), dma, dma((2,)), dma, dma((2,)),
+        dma, dma, dma, dma, dma,
     ]
     hbm = pl.BlockSpec(memory_space=pltpu.HBM)
     in_hbm = lambda x: pltpu.with_memory_space_constraint(x, pltpu.HBM)

time: 49.8 us -> 44.6 us (0.90)
  the two profiles are of different devices: /device:TPU:33 before, /device:TPU:40 now
where the time goes in v3:
time: 44.6 us; the launch traced here: 44.4 us
  Pallas kernels  43.2 us (97%)
  other arithmetic  1.25 us (3%)
    pallas_call x1, Pallas kernels, local(): pl.pallas_call(functools.partial(kernel, steps, layers, rows, n), out_sha...  43.2 us
    mul x1, other arithmetic, local(): out = log * inverse[None]  1.25 us

profile of v3, /device:TPU:40, one launch (start us, length us, event | category | flops | bytes accessed | tf_op | source)
XLA Modules:
  0.0 44.4 jit_solution(788100827920181283)
XLA Ops:
  0.0 43.2 %gradient.1 = (f32[3,1024,128]{2,1,0:T(8,128)S(1)}, f32[1,128]{1,0:T(1,128)S(1)}) custom-call(f32[7,1024,128]{2,1,0:T(8,128)} %bitcast.8, f32[7,1024,128]{2,1,0:T(8,128)} %bitcast.9, f32[3,1024,128]{2,1,0:T(8,128)} %bitcast.10, s32[1024,128]{1,0:T(8,128)} %bitcast.12, s32[3,1024,128]{2,1,0:T(8,128)} %bitcast.11), custom_call_target="tpu_custom_call" | custom-call | tf_op jit(solution)/shard_map/gradient/pallas_call | solution.py:393
  43.2 1.2 %broadcast_multiply_fusion = f32[3,1024,128]{2,1,0:T(8,128)} fusion(f32[3,1024,128]{2,1,0:T(8,128)S(1)} %get-tuple-element.7, f32[128]{0:T(128)S(1)} %bitcast.7), kind=kLoop, calls=%fused_computation | loop fusion | flops 393216 | bytes 3146240 | tf_op jit(solution)/shard_map/mul | solution.py:413

commit v4 on v3

--- a/solution.py
+++ b/solution.py
@@ -13,7 +13,8 @@
 epsilon = 1e-06
 
 PLANE = 8
-BLOCK = 32
+BLOCK = 64
+SHARED = 32
 
 
 def multiplier(codes):
@@ -39,16 +40,17 @@
     stage_factor, stage_perm, stage_low, stage_high, stage_ra, stage_rb, got_ra, got_rb,
     stage_sum, sums, stage_inv, got_inv,
     load_sem, send_up, recv_up, send_down, recv_down,
-    send_sum, recv_sum, send_inv, send_extra, recv_inv,
+    send_sum, recv_sum, send_inv, send_first, recv_inv,
 ):
     half = rows // 2
     cells = layers * rows
     top = cells - rows
     planes = n // PLANE
-    takers = 2 * PLANE - 1
+    takers = 2 * PLANE
     me = lax.axis_index("gx")
     first, last = me == 0, me == n - 1
-    taker = jnp.logical_and(me >= 1, me <= takers)
+    zero_takes = lax.axis_index("groups") != 0
+    taker = jnp.logical_and(me < takers, jnp.logical_or(me > 0, zero_takes))
     up, down = me + 1, me - 1
 
     def wait_rows(sem, row_count, wide=1):
@@ -68,6 +70,7 @@
         return [(src, dst, begin, end - begin) for src, dst in refs]
 
     load(0, span(fields, 0, half) + span(fields, top + half, cells))
+    load(1, span(fields, half, 2 * rows) + span(others, 0, 2 * rows))
 
     barrier = pltpu.get_barrier_semaphore()
 
@@ -149,14 +152,11 @@
         return jnp.where(condition, 1, 0)
 
     wait_rows(load_sem.at[0], 4 * steps * half, steps)
-    pl.semaphore_wait(barrier, 2 + takers - one_if(first) - one_if(last) - one_if(taker))
+    pl.semaphore_wait(barrier, 1 + takers + one_if(zero_takes) - one_if(first) - one_if(last) - one_if(taker))
     start_up(0, 1)
     start_down(0, 1)
 
-    load(1, span(fields, half, 2 * rows) + span(others, 0, 2 * rows))
     load(2, span(fields + others, 2 * rows, 4 * rows))
-    load(3, span(fields + others, 4 * rows, 6 * rows))
-    load(4, span(fields, 6 * rows, top + half) + span(others, 6 * rows, cells))
     edge = 2 * steps * (2 * rows - half) + 7 * 2 * rows
     whole = (2 * steps + 7) * 2 * rows
 
@@ -165,7 +165,7 @@
     z_open = jnp.where(lane == rows - 1, 0.0, 1.0).astype(F32)
 
     def fold(square):
-        return jnp.sum(square.reshape(BLOCK // 8, 8, rows), axis=0)
+        return jnp.sum(square.reshape(square.shape[0] // 8, 8, rows), axis=0)
 
     def block(start, in_layer, acc, from_below, to_above):
         at = pl.ds(start, BLOCK)
@@ -226,11 +226,13 @@
         return lax.fori_loop(begin, end, layer_of, acc)
 
     wait_rows(load_sem.at[1], edge, steps)
+    load(3, span(fields + others, 4 * rows, 6 * rows))
     stage_perm[...] = perm[0, low_a, :] * act[low_a, :].astype(F32)
     acc = layer_of(0, jnp.zeros((8, rows), F32), from_below=False)
     start_down(2)
     stage_low[...] = log_ref[0, low_a, :]
     wait_rows(load_sem.at[2], whole, steps)
+    load(4, span(fields, 6 * rows, top + half) + span(others, 6 * rows, cells))
     acc = middle(1, 3, acc)
     start_down(3)
     wait_rows(load_sem.at[3], whole, steps)
@@ -265,8 +267,8 @@
         return jnp.where(condition, value, 0.0)
 
     def shared(i, acc):
-        there = pl.ds(pl.multiple_of(i * BLOCK, BLOCK), BLOCK)
-        here = pl.ds(pl.multiple_of(top + i * BLOCK, BLOCK), BLOCK)
+        there = pl.ds(pl.multiple_of(i * SHARED, SHARED), SHARED)
+        here = pl.ds(pl.multiple_of(top + i * SHARED, SHARED), SHARED)
         inside = jnp.logical_not(last)
         products = products_of(pres, adj, here, above_pres, above_adj, there)
         factor = multiplier(code[0, here, :]) * act[here, :].astype(F32)
@@ -277,10 +279,10 @@
         reply = k_up * other
         stage_ra[there, :] = reply
         reply = keep(inside, reply + above_log[there, :])
-        end = keep(last, log_ref[0, pl.ds(pl.multiple_of(top + half + i * BLOCK, BLOCK), BLOCK), :])
+        end = keep(last, log_ref[0, pl.ds(pl.multiple_of(top + half + i * SHARED, SHARED), SHARED), :])
         acc = acc + fold(log * log) + fold(reply * reply) + fold(end * end)
 
-        here = pl.ds(pl.multiple_of(half + i * BLOCK, BLOCK), BLOCK)
+        here = pl.ds(pl.multiple_of(half + i * SHARED, SHARED), SHARED)
         inside = jnp.logical_not(first)
         products = products_of(below_pres, below_adj, there, pres, adj, here)
         factor = below_factor[there, :] * act[here, :].astype(F32)
@@ -294,23 +296,28 @@
         end = keep(first, log_ref[0, there, :])
         return acc + fold(log * log) + fold(reply * reply) + fold(end * end)
 
-    acc = lax.fori_loop(0, half // BLOCK, shared, acc)
+    acc = lax.fori_loop(0, half // SHARED, shared, acc)
 
     partial = jnp.sum(acc, axis=0, keepdims=True)
     stage_sum[...] = partial
-    to_takers = [remote(stage_sum, sums.at[me], send_sum, recv_sum, q) for q in range(1, takers + 1)]
+    to_takers = [remote(stage_sum, sums.at[me], send_sum.at[int(q == 0)], recv_sum, q) for q in range(takers)]
+    to_zero = jnp.logical_and(zero_takes, jnp.logical_not(first))
+
+    @pl.when(to_zero)
+    def _():
+        to_takers[0].start()
 
     @pl.when(jnp.logical_not(taker))
     def _():
-        for copy in to_takers:
+        for copy in to_takers[1:]:
             copy.start()
 
     @pl.when(taker)
     def _():
-        for q in range(1, takers + 1):
+        for q in range(1, takers):
             @pl.when(me != q)
             def _():
-                to_takers[q - 1].start()
+                to_takers[q].start()
 
     start_up(5)
     start_down(4)
@@ -327,9 +334,20 @@
         log_ref[0, top_b, :] += got_rb[...]
         wait_rows(send_up, (2 * steps + 4) * half, 2)
 
+    @pl.when(to_zero)
+    def _():
+        wait_rows(send_sum.at[1], 1)
+
+    @pl.when(jnp.logical_and(taker, jnp.logical_not(first)))
+    def _():
+        wait_rows(send_sum.at[0], takers - 2)
+
+    @pl.when(jnp.logical_or(first, jnp.logical_not(taker)))
+    def _():
+        wait_rows(send_sum.at[0], takers - 1)
+
     @pl.when(taker)
     def _():
-        wait_rows(send_sum, takers - 1)
         sums[me] = partial
         wait_rows(recv_sum, n - 1)
         quarter = n // 4
@@ -338,15 +356,16 @@
         entries = 3 * cells * rows * n
         inverse = jnp.broadcast_to(1.0 / jnp.sqrt(total / entries + epsilon), inv_ref.shape)
         inv_ref[...] = inverse
+        stage_inv[...] = inverse
 
         @pl.when(me >= PLANE)
         def _():
-            stage_inv[...] = inverse
             for z in range(1, planes - 1):
                 remote(stage_inv, got_inv, send_inv, recv_inv, me + z * PLANE).start()
-            to_first = remote(stage_inv, got_inv, send_extra, recv_inv, 0)
-
-            @pl.when(me == PLANE)
+            late = jnp.logical_and(me == takers - 1, jnp.logical_not(zero_takes))
+            to_first = remote(stage_inv, got_inv, send_first, recv_inv, 0)
+
+            @pl.when(late)
             def _():
                 to_first.start()
                 to_first.wait_send()
@@ -355,7 +374,6 @@
 
     @pl.when(jnp.logical_not(taker))
     def _():
-        wait_rows(send_sum, takers)
         wait_rows(recv_inv, 1)
         inv_ref[...] = got_inv[...]
 
@@ -386,7 +404,7 @@
         vmem((1, lanes), F32), vmem((n, 1, lanes), F32),
         vmem((1, lanes), F32), vmem((1, lanes), F32),
         dma((5,)), dma, dma((2,)), dma, dma((2,)),
-        dma, dma, dma, dma, dma,
+        dma((2,)), dma, dma, dma, dma,
     ]
     hbm = pl.BlockSpec(memory_space=pltpu.HBM)
     in_hbm = lambda x: pltpu.with_memory_space_constraint(x, pltpu.HBM)

time: 44.6 us -> 39.8 us (0.89)
  the two profiles are of different devices: /device:TPU:40 before, /device:TPU:33 now
where the time goes in v4:
time: 39.8 us; the launch traced here: 39.7 us
  Pallas kernels  38.5 us (97%)
  other arithmetic  1.25 us (3%)
    pallas_call x1, Pallas kernels, local(): pl.pallas_call(functools.partial(kernel, steps, layers, rows, n), out_sha...  38.5 us
    mul x1, other arithmetic, local(): out = log * inverse[None]  1.25 us

profile of v4, /device:TPU:33, one launch (start us, length us, event | category | flops | bytes accessed | tf_op | source)
XLA Modules:
  0.0 39.7 jit_solution(3715139951322395511)
XLA Ops:
  0.0 38.5 %gradient.1 = (f32[3,1024,128]{2,1,0:T(8,128)S(1)}, f32[1,128]{1,0:T(1,128)S(1)}) custom-call(f32[7,1024,128]{2,1,0:T(8,128)} %bitcast.8, f32[7,1024,128]{2,1,0:T(8,128)} %bitcast.9, f32[3,1024,128]{2,1,0:T(8,128)} %bitcast.10, s32[1024,128]{1,0:T(8,128)} %bitcast.12, s32[3,1024,128]{2,1,0:T(8,128)} %bitcast.11), custom_call_target="tpu_custom_call" | custom-call | tf_op jit(solution)/shard_map/gradient/pallas_call | solution.py:411
  38.5 1.2 %broadcast_multiply_fusion = f32[3,1024,128]{2,1,0:T(8,128)} fusion(f32[3,1024,128]{2,1,0:T(8,128)S(1)} %get-tuple-element.7, f32[128]{0:T(128)S(1)} %bitcast.7), kind=kLoop, calls=%fused_computation | loop fusion | flops 393216 | bytes 3146240 | tf_op jit(solution)/shard_map/mul | solution.py:431

commit v5 on v4

--- a/solution.py
+++ b/solution.py
@@ -14,7 +14,8 @@
 
 PLANE = 8
 BLOCK = 64
-SHARED = 32
+
+LOW = 56
 
 
 def multiplier(codes):
@@ -42,7 +43,7 @@
     load_sem, send_up, recv_up, send_down, recv_down,
     send_sum, recv_sum, send_inv, send_first, recv_inv,
 ):
-    half = rows // 2
+    high = rows - LOW
     cells = layers * rows
     top = cells - rows
     planes = n // PLANE
@@ -69,9 +70,6 @@
     def span(refs, begin, end):
         return [(src, dst, begin, end - begin) for src, dst in refs]
 
-    load(0, span(fields, 0, half) + span(fields, top + half, cells))
-    load(1, span(fields, half, 2 * rows) + span(others, 0, 2 * rows))
-
     barrier = pltpu.get_barrier_semaphore()
 
     def greet(device):
@@ -84,6 +82,9 @@
     @pl.when(jnp.logical_not(first))
     def _():
         greet(down)
+
+    load(0, span(fields, 0, LOW) + span(fields, top + LOW, cells))
+    load(1, span(fields, LOW, 2 * rows) + span(others, 0, 2 * rows))
 
     @pl.when(taker)
     def _():
@@ -105,8 +106,8 @@
     act[pl.ds(cells, 8), :] = jnp.zeros((8, rows), jnp.int32)
     to_up_y[pl.ds(0, 8), :] = zero8
 
-    low_a = pl.ds(0, half)
-    top_b = pl.ds(top + half, half)
+    low_a = pl.ds(0, LOW)
+    top_b = pl.ds(top + LOW, high)
 
     def remote(src, dst, send, recv, device):
         return pltpu.make_async_remote_copy(
@@ -151,13 +152,14 @@
     def one_if(condition):
         return jnp.where(condition, 1, 0)
 
-    wait_rows(load_sem.at[0], 4 * steps * half, steps)
+    wait_rows(load_sem.at[0], 2 * steps * rows, steps)
     pl.semaphore_wait(barrier, 1 + takers + one_if(zero_takes) - one_if(first) - one_if(last) - one_if(taker))
     start_up(0, 1)
     start_down(0, 1)
 
-    load(2, span(fields + others, 2 * rows, 4 * rows))
-    edge = 2 * steps * (2 * rows - half) + 7 * 2 * rows
+    load(2, span(fields, 6 * rows, top + LOW) + span(others, 6 * rows, cells))
+    first_two = 2 * steps * (2 * rows - LOW) + 7 * 2 * rows
+    last_two = 2 * steps * (rows + LOW) + 7 * 2 * rows
     whole = (2 * steps + 7) * 2 * rows
 
     lane = lax.broadcasted_iota(jnp.int32, (BLOCK, rows), 1)
@@ -225,27 +227,6 @@
     def middle(begin, end, acc):
         return lax.fori_loop(begin, end, layer_of, acc)
 
-    wait_rows(load_sem.at[1], edge, steps)
-    load(3, span(fields + others, 4 * rows, 6 * rows))
-    stage_perm[...] = perm[0, low_a, :] * act[low_a, :].astype(F32)
-    acc = layer_of(0, jnp.zeros((8, rows), F32), from_below=False)
-    start_down(2)
-    stage_low[...] = log_ref[0, low_a, :]
-    wait_rows(load_sem.at[2], whole, steps)
-    load(4, span(fields, 6 * rows, top + half) + span(others, 6 * rows, cells))
-    acc = middle(1, 3, acc)
-    start_down(3)
-    wait_rows(load_sem.at[3], whole, steps)
-    acc = middle(3, 5, acc)
-    wait_rows(load_sem.at[4], edge, steps)
-    start_up(2)
-    stage_factor[...] = multiplier(code[0, top_b, :]) * act[top_b, :].astype(F32)
-    acc = middle(5, layers - 1, acc)
-    start_up(3)
-    stage_high[...] = perm[0, top_b, :] * to_up_x[top_b, :]
-    acc = layer_of(layers - 1, acc, to_above=False)
-    start_up(4)
-
     def products_of(lower_pres, lower_adj, lower_at, upper_pres, upper_adj, upper_at):
         total = None
         for t in range(steps):
@@ -255,48 +236,70 @@
             total = term if t == 0 else total + term
         return total
 
+    wait_rows(load_sem.at[1], first_two, steps)
+    load(3, span(fields + others, 2 * rows, 4 * rows))
+    stage_perm[...] = perm[0, low_a, :] * act[low_a, :].astype(F32)
+    acc = layer_of(0, jnp.zeros((8, rows), F32), from_below=False)
+    start_down(2)
+    stage_low[...] = log_ref[0, low_a, :]
+
+    wait_rows(load_sem.at[2], last_two, steps)
+    load(4, span(fields + others, 4 * rows, 6 * rows))
+    start_up(2)
+    start_down(3)
+    under = pl.ds(top - rows + LOW, high)
+    products = products_of(pres, adj, under, pres, adj, top_b)
+    opened = act[top_b, :].astype(F32)
+    stage_factor[...] = multiplier(code[0, top_b, :]) * opened
+    factor = multiplier(code[0, under, :]) * act[under, :].astype(F32) * opened
+    stage_high[...] = perm[0, top_b, :] * face(products, factor, perm[0, under, :], perm[0, top_b, :])[1]
+
+    wait_rows(load_sem.at[3], whole, steps)
+    acc = layer_of(1, acc)
+    start_up(3, 4)
+    acc = layer_of(2, acc)
+    wait_rows(load_sem.at[4], whole, steps)
+    acc = middle(3, layers - 1, acc)
+    acc = layer_of(layers - 1, acc, to_above=False)
+
     @pl.when(jnp.logical_not(last))
     def _():
-        wait_rows(recv_down.at[0], (2 * steps + 2) * half, 2)
+        wait_rows(recv_down.at[0], (2 * steps + 2) * LOW, 2)
 
     @pl.when(jnp.logical_not(first))
     def _():
-        wait_rows(recv_up.at[0], (2 * steps + 3) * half, 2)
+        wait_rows(recv_up.at[0], (2 * steps + 3) * high, 2)
 
     def keep(condition, value):
         return jnp.where(condition, value, 0.0)
 
-    def shared(i, acc):
-        there = pl.ds(pl.multiple_of(i * SHARED, SHARED), SHARED)
-        here = pl.ds(pl.multiple_of(top + i * SHARED, SHARED), SHARED)
-        inside = jnp.logical_not(last)
-        products = products_of(pres, adj, here, above_pres, above_adj, there)
-        factor = multiplier(code[0, here, :]) * act[here, :].astype(F32)
-        k, k_up = perm[0, here, :], above_perm[there, :]
-        mine, other = face(products, factor, k, k_up)
-        log = log_ref[0, here, :] + keep(inside, k * mine)
-        log_ref[0, here, :] = log
-        reply = k_up * other
-        stage_ra[there, :] = reply
-        reply = keep(inside, reply + above_log[there, :])
-        end = keep(last, log_ref[0, pl.ds(pl.multiple_of(top + half + i * SHARED, SHARED), SHARED), :])
-        acc = acc + fold(log * log) + fold(reply * reply) + fold(end * end)
-
-        here = pl.ds(pl.multiple_of(half + i * SHARED, SHARED), SHARED)
-        inside = jnp.logical_not(first)
-        products = products_of(below_pres, below_adj, there, pres, adj, here)
-        factor = below_factor[there, :] * act[here, :].astype(F32)
-        k, k_low = perm[0, here, :], below_perm[there, :]
-        other, mine = face(products, factor, k_low, k)
-        log = log_ref[0, here, :] + keep(inside, k * mine)
-        log_ref[0, here, :] = log
-        reply = k_low * other
-        stage_rb[there, :] = reply
-        reply = keep(inside, reply + below_log[there, :])
-        end = keep(first, log_ref[0, there, :])
-        return acc + fold(log * log) + fold(reply * reply) + fold(end * end)
-
-    acc = lax.fori_loop(0, half // SHARED, shared, acc)
+    everything, here = pl.ds(0, LOW), pl.ds(top, LOW)
+    inside = jnp.logical_not(last)
+    products = products_of(pres, adj, here, above_pres, above_adj, everything)
+    factor = multiplier(code[0, here, :]) * act[here, :].astype(F32)
+    k, k_up = perm[0, here, :], above_perm[...]
+    mine, other = face(products, factor, k, k_up)
+    log = log_ref[0, here, :] + keep(inside, k * mine)
+    log_ref[0, here, :] = log
+    reply = k_up * other
+    stage_ra[...] = reply
+    reply = keep(inside, reply + above_log[...])
+    end = keep(last, log_ref[0, top_b, :])
+    acc = acc + fold(log * log) + fold(reply * reply) + fold(end * end)
+
+    everything, here = pl.ds(0, high), pl.ds(LOW, high)
+    inside = jnp.logical_not(first)
+    products = products_of(below_pres, below_adj, everything, pres, adj, here)
+    factor = below_factor[...] * act[here, :].astype(F32)
+    k, k_low = perm[0, here, :], below_perm[...]
+    other, mine = face(products, factor, k_low, k)
+    log = log_ref[0, here, :] + keep(inside, k * mine)
+    log_ref[0, here, :] = log
+    reply = k_low * other
+    stage_rb[...] = reply
+    reply = keep(inside, reply + below_log[...])
+    end = keep(first, log_ref[0, low_a, :])
+    acc = acc + fold(log * log) + fold(reply * reply) + fold(end * end)
 
     partial = jnp.sum(acc, axis=0, keepdims=True)
     stage_sum[...] = partial
@@ -324,15 +327,15 @@
 
     @pl.when(jnp.logical_not(first))
     def _():
-        wait_rows(recv_up.at[1], half)
+        wait_rows(recv_up.at[1], LOW)
         log_ref[0, low_a, :] += got_ra[...]
-        wait_rows(send_down, (2 * steps + 3) * half, 2)
+        wait_rows(send_down, (2 * steps + 2) * LOW + high, 2)
 
     @pl.when(jnp.logical_not(last))
     def _():
-        wait_rows(recv_down.at[1], half)
+        wait_rows(recv_down.at[1], high)
         log_ref[0, top_b, :] += got_rb[...]
-        wait_rows(send_up, (2 * steps + 4) * half, 2)
+        wait_rows(send_up, (2 * steps + 3) * high + LOW, 2)
 
     @pl.when(to_zero)
     def _():
@@ -381,15 +384,10 @@
 def local(n, pressure, adjoint, permeability, active, fault_codes):
     steps, layers, rows, lanes = pressure.shape
     cells = layers * rows
-    half = rows // 2
+    high = rows - LOW
     planes = n // PLANE
     vmem, dma = pltpu.VMEM, pltpu.SemaphoreType.DMA
-    halo = [
-        vmem((steps, half, lanes), F32),
-        vmem((steps, half, lanes), F32),
-        vmem((half, lanes), F32),
-    ]
-    tile = vmem((half, lanes), F32)
+    low_tile, high_tile = vmem((LOW, lanes), F32), vmem((high, lanes), F32)
     scratch = [
         vmem((steps, cells + 8, lanes), F32),
         vmem((steps, cells + 8, lanes), F32),
@@ -398,9 +396,9 @@
         vmem((3, cells, lanes), jnp.int32),
         vmem((cells, lanes), F32),
         vmem((cells + 8, lanes), F32),
-        *halo, tile,
-        *halo, tile, tile,
-        tile, tile, tile, tile, tile, tile, tile, tile,
+        vmem((steps, LOW, lanes), F32), vmem((steps, LOW, lanes), F32), low_tile, low_tile,
+        vmem((steps, high, lanes), F32), vmem((steps, high, lanes), F32), high_tile, high_tile, high_tile,
+        high_tile, low_tile, low_tile, high_tile, low_tile, high_tile, low_tile, high_tile,
         vmem((1, lanes), F32), vmem((n, 1, lanes), F32),
         vmem((1, lanes), F32), vmem((1, lanes), F32),
         dma((5,)), dma, dma((2,)), dma, dma((2,)),

time: 39.8 us -> 39 us (0.980)
  Pallas kernels: 38.5 us -> 37.7 us
    pallas_call x1, Pallas kernels: 38.5 us -> 37.7 us  [local(): pl.pallas_call(functools.partial(kernel, steps, layers, rows, n), out_sha...]
where the time goes in v5:
time: 39 us; the launch traced here: 38.9 us
  Pallas kernels  37.7 us (97%)
  other arithmetic  1.25 us (3%)
    pallas_call x1, Pallas kernels, local(): pl.pallas_call(functools.partial(kernel, steps, layers, rows, n), out_sha...  37.7 us
    mul x1, other arithmetic, local(): out = log * inverse[None]  1.25 us

profile of v5, /device:TPU:33, one launch (start us, length us, event | category | flops | bytes accessed | tf_op | source)
XLA Modules:
  0.0 38.9 jit_solution(3392824239839062660)
XLA Ops:
  0.0 37.7 %gradient.1 = (f32[3,1024,128]{2,1,0:T(8,128)S(1)}, f32[1,128]{1,0:T(1,128)S(1)}) custom-call(f32[7,1024,128]{2,1,0:T(8,128)} %bitcast.8, f32[7,1024,128]{2,1,0:T(8,128)} %bitcast.9, f32[3,1024,128]{2,1,0:T(8,128)} %bitcast.10, s32[1024,128]{1,0:T(8,128)} %bitcast.12, s32[3,1024,128]{2,1,0:T(8,128)} %bitcast.11), custom_call_target="tpu_custom_call" | custom-call | tf_op jit(solution)/shard_map/gradient/pallas_call | solution.py:409
  37.7 1.2 %broadcast_multiply_fusion = f32[3,1024,128]{2,1,0:T(8,128)} fusion(f32[3,1024,128]{2,1,0:T(8,128)S(1)} %get-tuple-element.7, f32[128]{0:T(128)S(1)} %bitcast.7), kind=kLoop, calls=%fused_computation | loop fusion | flops 393216 | bytes 3146240 | tf_op jit(solution)/shard_map/mul | solution.py:429

commit v6 on v5

--- a/solution.py
+++ b/solution.py
@@ -34,16 +34,24 @@
     steps, layers, rows, n,
     pres_hbm, adj_hbm, perm_hbm, act_hbm, code_hbm,
     log_ref, inv_ref,
-    pres, adj, perm, act, code,
+    both, perm, act, code,
     to_up_x, to_up_y,
-    above_pres, above_adj, above_perm, above_log,
-    below_pres, below_adj, below_perm, below_factor, below_log,
-    stage_factor, stage_perm, stage_low, stage_high, stage_ra, stage_rb, got_ra, got_rb,
+    above_both, above_rest, below_both, below_rest,
+    stage_down, stage_up, stage_ra, stage_rb, got_ra, got_rb,
     stage_sum, sums, stage_inv, got_inv,
     load_sem, send_up, recv_up, send_down, recv_down,
     send_sum, recv_sum, send_inv, send_first, recv_inv,
 ):
     high = rows - LOW
+
+    def halves(ref):
+        return ref.at[pl.ds(0, steps)], ref.at[pl.ds(steps, steps)]
+
+    pres, adj = halves(both)
+    above_pres, above_adj = halves(above_both)
+    below_pres, below_adj = halves(below_both)
+    above_perm, above_log = above_rest.at[0], above_rest.at[1]
+    below_perm, below_factor, below_log = (below_rest.at[i] for i in range(3))
     cells = layers * rows
     top = cells - rows
     planes = n // PLANE
@@ -55,7 +63,7 @@
     up, down = me + 1, me - 1
 
     def wait_rows(sem, row_count, wide=1):
-        ref = pres.at[pl.ds(0, wide), pl.ds(0, row_count // wide)]
+        ref = both.at[pl.ds(0, wide), pl.ds(0, row_count // wide)]
         pltpu.make_async_copy(ref, ref, sem).wait()
 
     def load(group, parts):
@@ -70,6 +78,10 @@
     def span(refs, begin, end):
         return [(src, dst, begin, end - begin) for src, dst in refs]
 
+    load(0, span(fields, top + LOW, cells))
+    load(5, span(fields, 0, LOW))
+    load(1, span(fields, LOW, 2 * rows) + span(others, 0, 2 * rows))
+
     barrier = pltpu.get_barrier_semaphore()
 
     def greet(device):
@@ -82,9 +94,6 @@
     @pl.when(jnp.logical_not(first))
     def _():
         greet(down)
-
-    load(0, span(fields, 0, LOW) + span(fields, top + LOW, cells))
-    load(1, span(fields, LOW, 2 * rows) + span(others, 0, 2 * rows))
 
     @pl.when(taker)
     def _():
@@ -116,25 +125,12 @@
         )
 
     goes_down = [
-        remote(s, d, send_down, recv_down.at[int(i == 4)], down)
-        for i, (s, d) in enumerate([
-            (pres.at[:, low_a], above_pres),
-            (adj.at[:, low_a], above_adj),
-            (stage_perm, above_perm),
-            (stage_low, above_log),
-            (stage_rb, got_rb),
-        ])
+        remote(s, d, send_down, recv_down.at[int(i == 2)], down)
+        for i, (s, d) in enumerate([(both.at[:, low_a], above_both), (stage_down, above_rest), (stage_rb, got_rb)])
     ]
     goes_up = [
-        remote(s, d, send_up, recv_up.at[int(i == 5)], up)
-        for i, (s, d) in enumerate([
-            (pres.at[:, top_b], below_pres),
-            (adj.at[:, top_b], below_adj),
-            (perm.at[0, top_b], below_perm),
-            (stage_factor, below_factor),
-            (stage_high, below_log),
-            (stage_ra, got_ra),
-        ])
+        remote(s, d, send_up, recv_up.at[int(i == 2)], up)
+        for i, (s, d) in enumerate([(both.at[:, top_b], below_both), (stage_up, below_rest), (stage_ra, got_ra)])
     ]
 
     def start_up(*parts):
@@ -152,10 +148,11 @@
     def one_if(condition):
         return jnp.where(condition, 1, 0)
 
-    wait_rows(load_sem.at[0], 2 * steps * rows, steps)
+    wait_rows(load_sem.at[0], 2 * steps * high, steps)
     pl.semaphore_wait(barrier, 1 + takers + one_if(zero_takes) - one_if(first) - one_if(last) - one_if(taker))
-    start_up(0, 1)
-    start_down(0, 1)
+    start_up(0)
+    wait_rows(load_sem.at[5], 2 * steps * LOW, steps)
+    start_down(0)
 
     load(2, span(fields, 6 * rows, top + LOW) + span(others, 6 * rows, cells))
     first_two = 2 * steps * (2 * rows - LOW) + 7 * 2 * rows
@@ -238,25 +235,24 @@
 
     wait_rows(load_sem.at[1], first_two, steps)
     load(3, span(fields + others, 2 * rows, 4 * rows))
-    stage_perm[...] = perm[0, low_a, :] * act[low_a, :].astype(F32)
+    stage_down[0] = perm[0, low_a, :] * act[low_a, :].astype(F32)
     acc = layer_of(0, jnp.zeros((8, rows), F32), from_below=False)
-    start_down(2)
-    stage_low[...] = log_ref[0, low_a, :]
+    stage_down[1] = log_ref[0, low_a, :]
 
     wait_rows(load_sem.at[2], last_two, steps)
     load(4, span(fields + others, 4 * rows, 6 * rows))
-    start_up(2)
-    start_down(3)
+    start_down(1)
+    stage_up[0] = perm[0, top_b, :]
     under = pl.ds(top - rows + LOW, high)
     products = products_of(pres, adj, under, pres, adj, top_b)
     opened = act[top_b, :].astype(F32)
-    stage_factor[...] = multiplier(code[0, top_b, :]) * opened
+    stage_up[1] = multiplier(code[0, top_b, :]) * opened
     factor = multiplier(code[0, under, :]) * act[under, :].astype(F32) * opened
-    stage_high[...] = perm[0, top_b, :] * face(products, factor, perm[0, under, :], perm[0, top_b, :])[1]
+    stage_up[2] = perm[0, top_b, :] * face(products, factor, perm[0, under, :], perm[0, top_b, :])[1]
 
     wait_rows(load_sem.at[3], whole, steps)
     acc = layer_of(1, acc)
-    start_up(3, 4)
+    start_up(1)
     acc = layer_of(2, acc)
     wait_rows(load_sem.at[4], whole, steps)
     acc = middle(3, layers - 1, acc)
@@ -265,10 +261,6 @@
     @pl.when(jnp.logical_not(last))
     def _():
         wait_rows(recv_down.at[0], (2 * steps + 2) * LOW, 2)
-
-    @pl.when(jnp.logical_not(first))
-    def _():
-        wait_rows(recv_up.at[0], (2 * steps + 3) * high, 2)
 
     def keep(condition, value):
         return jnp.where(condition, value, 0.0)
@@ -287,6 +279,10 @@
     end = keep(last, log_ref[0, top_b, :])
     acc = acc + fold(log * log) + fold(reply * reply) + fold(end * end)
 
+    @pl.when(jnp.logical_not(first))
+    def _():
+        wait_rows(recv_up.at[0], (2 * steps + 3) * high, 2)
+
     everything, here = pl.ds(0, high), pl.ds(LOW, high)
     inside = jnp.logical_not(first)
     products = products_of(below_pres, below_adj, everything, pres, adj, here)
@@ -322,8 +318,8 @@
             def _():
                 to_takers[q].start()
 
-    start_up(5)
-    start_down(4)
+    start_up(2)
+    start_down(2)
 
     @pl.when(jnp.logical_not(first))
     def _():
@@ -389,19 +385,19 @@
     vmem, dma = pltpu.VMEM, pltpu.SemaphoreType.DMA
     low_tile, high_tile = vmem((LOW, lanes), F32), vmem((high, lanes), F32)
     scratch = [
-        vmem((steps, cells + 8, lanes), F32),
-        vmem((steps, cells + 8, lanes), F32),
+        vmem((2 * steps, cells + 8, lanes), F32),
         vmem((3, cells + 8, lanes), F32),
         vmem((cells + 8, lanes), jnp.int32),
         vmem((3, cells, lanes), jnp.int32),
         vmem((cells, lanes), F32),
         vmem((cells + 8, lanes), F32),
-        vmem((steps, LOW, lanes), F32), vmem((steps, LOW, lanes), F32), low_tile, low_tile,
-        vmem((steps, high, lanes), F32), vmem((steps, high, lanes), F32), high_tile, high_tile, high_tile,
-        high_tile, low_tile, low_tile, high_tile, low_tile, high_tile, low_tile, high_tile,
+        vmem((2 * steps, LOW, lanes), F32), vmem((2, LOW, lanes), F32),
+        vmem((2 * steps, high, lanes), F32), vmem((3, high, lanes), F32),
+        vmem((2, LOW, lanes), F32), vmem((3, high, lanes), F32),
+        low_tile, high_tile, low_tile, high_tile,
         vmem((1, lanes), F32), vmem((n, 1, lanes), F32),
         vmem((1, lanes), F32), vmem((1, lanes), F32),
-        dma((5,)), dma, dma((2,)), dma, dma((2,)),
+        dma((6,)), dma, dma((2,)), dma, dma((2,)),
         dma((2,)), dma, dma, dma, dma,
     ]
     hbm = pl.BlockSpec(memory_space=pltpu.HBM)

time: 39 us -> 39.1 us (level)
  no operation moved by 1% of the time
where the time goes in v6:
time: 39.1 us; the launch traced here: 39 us
  Pallas kernels  37.7 us (96%)
  other arithmetic  1.25 us (3%)
    pallas_call x1, Pallas kernels, local(): pl.pallas_call(functools.partial(kernel, steps, layers, rows, n), out_sha...  37.7 us
    mul x1, other arithmetic, local(): out = log * inverse[None]  1.25 us

profile of v6, /device:TPU:33, one launch (start us, length us, event | category | flops | bytes accessed | tf_op | source)
XLA Modules:
  0.0 39.0 jit_solution(3062777661268685204)
XLA Ops:
  0.0 37.7 %gradient.1 = (f32[3,1024,128]{2,1,0:T(8,128)S(1)}, f32[1,128]{1,0:T(1,128)S(1)}) custom-call(f32[7,1024,128]{2,1,0:T(8,128)} %bitcast.8, f32[7,1024,128]{2,1,0:T(8,128)} %bitcast.9, f32[3,1024,128]{2,1,0:T(8,128)} %bitcast.10, s32[1024,128]{1,0:T(8,128)} %bitcast.12, s32[3,1024,128]{2,1,0:T(8,128)} %bitcast.11), custom_call_target="tpu_custom_call" | custom-call | tf_op jit(solution)/shard_map/gradient/pallas_call | solution.py:405
  37.7 1.2 %broadcast_multiply_fusion = f32[3,1024,128]{2,1,0:T(8,128)} fusion(f32[3,1024,128]{2,1,0:T(8,128)S(1)} %get-tuple-element.7, f32[128]{0:T(128)S(1)} %bitcast.7), kind=kLoop, calls=%fused_computation | loop fusion | flops 393216 | bytes 3146240 | tf_op jit(solution)/shard_map/mul | solution.py:425

commit v7 on v6

--- a/solution.py
+++ b/solution.py
@@ -16,6 +16,8 @@
 BLOCK = 64
 
 LOW = 56
+
+PIECES = 6
 
 
 def multiplier(codes):
@@ -375,6 +377,20 @@
     def _():
         wait_rows(recv_inv, 1)
         inv_ref[...] = got_inv[...]
+
+
+def scale(log_ref, inv_ref, out_hbm, scaled, sem):
+    inverse = inv_ref[...]
+    rows = log_ref.shape[1] // (PIECES // 3)
+    copies = []
+    for i in range(PIECES):
+        d, at = i // (PIECES // 3), pl.ds(i % (PIECES // 3) * rows, rows)
+        scaled[d, at, :] = log_ref[d, at, :] * inverse
+        copy = pltpu.make_async_copy(scaled.at[d, at], out_hbm.at[d, at], sem.at[i])
+        copy.start()
+        copies.append(copy)
+    for copy in copies:
+        copy.wait()
 
 
 def local(n, pressure, adjoint, permeability, active, fault_codes):
@@ -422,7 +438,15 @@
         in_hbm(active.reshape(cells, lanes)),
         in_hbm(fault_codes.reshape(3, cells, lanes)),
     )
-    out = log * inverse[None]
+    out = pl.pallas_call(
+        scale,
+        out_shape=jax.ShapeDtypeStruct(log.shape, F32),
+        in_specs=[pl.BlockSpec(memory_space=pltpu.VMEM)] * 2,
+        out_specs=pl.BlockSpec(memory_space=pltpu.HBM),
+        scratch_shapes=[vmem(log.shape, F32), dma((PIECES,))],
+        compiler_params=pltpu.CompilerParams(vmem_limit_bytes=8 * 1024 * 1024),
+        name="scale",
+    )(log, inverse)
     return out.reshape(3, layers, rows, lanes)
 
 

time: 39.1 us -> 39 us (level)
  other arithmetic: 1.25 us -> 0 us
  Pallas kernels: 37.7 us -> 38.9 us
    mul x1 -> x0, other arithmetic: 1.25 us -> none  [local(): out = log * inverse[None]]
    pallas_call x0 -> x1, Pallas kernels: none -> 1.21 us  [local(): pl.pallas_call(scale, out_shape=jax.ShapeDtypeStruct(log.shape, F32), in_...]
where the time goes in v7:
time: 39 us; the launch traced here: 38.9 us
  Pallas kernels  38.9 us (100%)
    pallas_call x1, Pallas kernels, local(): pl.pallas_call(functools.partial(kernel, steps, layers, rows, n), out_sha...  37.7 us
    pallas_call x1, Pallas kernels, local(): pl.pallas_call(scale, out_shape=jax.ShapeDtypeStruct(log.shape, F32), in_...  1.21 us

profile of v7, /device:TPU:33, one launch (start us, length us, event | category | flops | bytes accessed | tf_op | source)
XLA Modules:
  0.0 38.9 jit_solution(5455955885082045656)
XLA Ops:
  0.0 37.7 %gradient.1 = (f32[3,1024,128]{2,1,0:T(8,128)S(1)}, f32[1,128]{1,0:T(1,128)S(1)}) custom-call(f32[7,1024,128]{2,1,0:T(8,128)} %bitcast.6, f32[7,1024,128]{2,1,0:T(8,128)} %bitcast.7, f32[3,1024,128]{2,1,0:T(8,128)} %bitcast.8, s32[1024,128]{1,0:T(8,128)} %bitcast.10, s32[3,1024,128]{2,1,0:T(8,128)} %bitcast.9), custom_call_target="tpu_custom_call" | custom-call | tf_op jit(solution)/shard_map/gradient/pallas_call | solution.py:421
  37.7 1.2 %scale.1 = f32[3,1024,128]{2,1,0:T(8,128)} custom-call(f32[3,1024,128]{2,1,0:T(8,128)S(1)} %get-tuple-element.7.log_ref, f32[1,128]{1,0:T(1,128)S(1)} %get-tuple-element.8.inv_ref), custom_call_target="tpu_custom_call" | custom-call | tf_op jit(solution)/shard_map/scale/pallas_call | solution.py:441

commit v8 on v7

--- a/solution.py
+++ b/solution.py
@@ -21,12 +21,12 @@
 
 
 def multiplier(codes):
-    return jnp.where(codes == 0, 1.0, jnp.where(codes == 1, 0.6, jnp.where(codes == 2, 0.25, 0.05)))
+    return jnp.where(codes == 0, 2.0, jnp.where(codes == 1, 1.2, jnp.where(codes == 2, 0.5, 0.1)))
 
 
 def face(products, factor, lower_perm, upper_perm):
     inverse = 1.0 / (lower_perm + upper_perm)
-    weight = (2.0 * factor) * products
+    weight = factor * products
     upper = upper_perm * inverse
     lower = lower_perm * inverse
     return weight * upper * upper, weight * lower * lower
@@ -42,7 +42,7 @@
     stage_down, stage_up, stage_ra, stage_rb, got_ra, got_rb,
     stage_sum, sums, stage_inv, got_inv,
     load_sem, send_up, recv_up, send_down, recv_down,
-    send_sum, recv_sum, send_inv, send_first, recv_inv,
+    send_sum, recv_sum, send_inv, send_first, recv_inv, partner,
 ):
     high = rows - LOW
 
@@ -89,11 +89,14 @@
     def greet(device):
         pl.semaphore_signal(barrier, inc=1, device_id={"gx": device}, device_id_type=MESH)
 
+    even = lax.rem(me, 2) == 0
+    odd = jnp.logical_not(even)
+
     @pl.when(jnp.logical_not(last))
     def _():
         greet(up)
 
-    @pl.when(jnp.logical_not(first))
+    @pl.when(jnp.logical_and(even, jnp.logical_not(first)))
     def _():
         greet(down)
 
@@ -127,11 +130,11 @@
         )
 
     goes_down = [
-        remote(s, d, send_down, recv_down.at[int(i == 2)], down)
+        remote(s, d, send_down, recv_down.at[i], down)
         for i, (s, d) in enumerate([(both.at[:, low_a], above_both), (stage_down, above_rest), (stage_rb, got_rb)])
     ]
     goes_up = [
-        remote(s, d, send_up, recv_up.at[int(i == 2)], up)
+        remote(s, d, send_up, recv_up.at[i], up)
         for i, (s, d) in enumerate([(both.at[:, top_b], below_both), (stage_up, below_rest), (stage_ra, got_ra)])
     ]
 
@@ -151,12 +154,22 @@
         return jnp.where(condition, 1, 0)
 
     wait_rows(load_sem.at[0], 2 * steps * high, steps)
-    pl.semaphore_wait(barrier, 1 + takers + one_if(zero_takes) - one_if(first) - one_if(last) - one_if(taker))
-    start_up(0)
+    pl.semaphore_wait(barrier, takers + one_if(odd) + one_if(zero_takes) - one_if(first) - one_if(last) - one_if(taker))
+    @pl.when(odd)
+    def _():
+        pl.semaphore_signal(partner, inc=1, device_id={"gx": down}, device_id_type=MESH)
+        start_up(0)
+
     wait_rows(load_sem.at[5], 2 * steps * LOW, steps)
     start_down(0)
 
     load(2, span(fields, 6 * rows, top + LOW) + span(others, 6 * rows, cells))
+
+    @pl.when(even)
+    def _():
+        pl.semaphore_wait(partner, 1)
+        start_up(0)
+
     first_two = 2 * steps * (2 * rows - LOW) + 7 * 2 * rows
     last_two = 2 * steps * (rows + LOW) + 7 * 2 * rows
     whole = (2 * steps + 7) * 2 * rows
@@ -262,7 +275,7 @@
 
     @pl.when(jnp.logical_not(last))
     def _():
-        wait_rows(recv_down.at[0], (2 * steps + 2) * LOW, 2)
+        wait_rows(recv_down.at[0], 2 * steps * LOW, 2)
 
     def keep(condition, value):
         return jnp.where(condition, value, 0.0)
@@ -270,6 +283,11 @@
     everything, here = pl.ds(0, LOW), pl.ds(top, LOW)
     inside = jnp.logical_not(last)
     products = products_of(pres, adj, here, above_pres, above_adj, everything)
+
+    @pl.when(jnp.logical_not(last))
+    def _():
+        wait_rows(recv_down.at[1], 2 * LOW, 2)
+
     factor = multiplier(code[0, here, :]) * act[here, :].astype(F32)
     k, k_up = perm[0, here, :], above_perm[...]
     mine, other = face(products, factor, k, k_up)
@@ -283,11 +301,16 @@
 
     @pl.when(jnp.logical_not(first))
     def _():
-        wait_rows(recv_up.at[0], (2 * steps + 3) * high, 2)
+        wait_rows(recv_up.at[0], 2 * steps * high, 2)
 
     everything, here = pl.ds(0, high), pl.ds(LOW, high)
     inside = jnp.logical_not(first)
     products = products_of(below_pres, below_adj, everything, pres, adj, here)
+
+    @pl.when(jnp.logical_not(first))
+    def _():
+        wait_rows(recv_up.at[1], 3 * high, 1)
+
     factor = below_factor[...] * act[here, :].astype(F32)
     k, k_low = perm[0, here, :], below_perm[...]
     other, mine = face(products, factor, k_low, k)
@@ -325,13 +348,13 @@
 
     @pl.when(jnp.logical_not(first))
     def _():
-        wait_rows(recv_up.at[1], LOW)
+        wait_rows(recv_up.at[2], LOW)
         log_ref[0, low_a, :] += got_ra[...]
         wait_rows(send_down, (2 * steps + 2) * LOW + high, 2)
 
     @pl.when(jnp.logical_not(last))
     def _():
-        wait_rows(recv_down.at[1], high)
+        wait_rows(recv_down.at[2], high)
         log_ref[0, top_b, :] += got_rb[...]
         wait_rows(send_up, (2 * steps + 3) * high + LOW, 2)
 
@@ -413,8 +436,8 @@
         low_tile, high_tile, low_tile, high_tile,
         vmem((1, lanes), F32), vmem((n, 1, lanes), F32),
         vmem((1, lanes), F32), vmem((1, lanes), F32),
-        dma((6,)), dma, dma((2,)), dma, dma((2,)),
-        dma((2,)), dma, dma, dma, dma,
+        dma((6,)), dma, dma((3,)), dma, dma((3,)),
+        dma((2,)), dma, dma, dma, dma, pltpu.SemaphoreType.REGULAR,
     ]
     hbm = pl.BlockSpec(memory_space=pltpu.HBM)
     in_hbm = lambda x: pltpu.with_memory_space_constraint(x, pltpu.HBM)

time: 39 us -> 39 us (level)
  no operation moved by 1% of the time
where the time goes in v8:
time: 39 us; the launch traced here: 38.9 us
  Pallas kernels  38.9 us (100%)
    pallas_call x1, Pallas kernels, local(): pl.pallas_call(functools.partial(kernel, steps, layers, rows, n), out_sha...  37.7 us
    pallas_call x1, Pallas kernels, local(): pl.pallas_call(scale, out_shape=jax.ShapeDtypeStruct(log.shape, F32), in_...  1.21 us

profile of v8, /device:TPU:33, one launch (start us, length us, event | category | flops | bytes accessed | tf_op | source)
XLA Modules:
  0.0 38.9 jit_solution(2061758741243575439)
XLA Ops:
  0.0 37.7 %gradient.1 = (f32[3,1024,128]{2,1,0:T(8,128)S(1)}, f32[1,128]{1,0:T(1,128)S(1)}) custom-call(f32[7,1024,128]{2,1,0:T(8,128)} %bitcast.6, f32[7,1024,128]{2,1,0:T(8,128)} %bitcast.7, f32[3,1024,128]{2,1,0:T(8,128)} %bitcast.8, s32[1024,128]{1,0:T(8,128)} %bitcast.10, s32[3,1024,128]{2,1,0:T(8,128)} %bitcast.9), custom_call_target="tpu_custom_call" | custom-call | tf_op jit(solution)/shard_map/gradient/pallas_call | solution.py:444
  37.7 1.2 %scale.1 = f32[3,1024,128]{2,1,0:T(8,128)} custom-call(f32[3,1024,128]{2,1,0:T(8,128)S(1)} %get-tuple-element.7.log_ref, f32[1,128]{1,0:T(1,128)S(1)} %get-tuple-element.8.inv_ref), custom_call_target="tpu_custom_call" | custom-call | tf_op jit(solution)/shard_map/scale/pallas_call | solution.py:464
